TPU v7x, 32 devices: a whole 2x2x4 slice. The times are simulated.
32 devices in a mesh: shear: 16 (over z, y, x), cross: 2 (over core).
Axes of the slice: x: 2, y: 2, z: 4, core: 2. Of those that a mesh axis runs over, the one named last changes fastest.
Arguments:
- positions: float32 [3, 16, 16, 2, 256], P(None, 'shear', None, 'cross'), may hold values from 0 to 1
- masses: float32 [16, 16, 2, 256], P('shear', None, 'cross'), may hold values from 0.002 to 0.008
- counts: int32 [16, 16, 2], P('shear', None, 'cross'), may hold values from 32 to 256
- shear_offset: int32 [1], replicated, may hold values from 0 to 15
Outputs:
- density: float32 [16, 16, 2, 256], P('shear', None, 'cross')
Inputs may be any that keep to these rules, and one draw needn't show every extreme that they name: `shear_offset`: a whole number of cells.
All inputs are finite; a program needn't handle non-finite values.
Results may differ from a plain program's by a relative error of at most 0.0003.
Values sent between devices are 32-bit elements; how exact they have to be, the bound alone decides.
A program may use at most 64 MiB of HBM per device.

v0:
```python
import jax
import jax.numpy as jnp
from jax import lax
from jax.sharding import PartitionSpec as P


def extended_2(block, sides, width):
    for axis, dim in sides:
        count = lax.axis_size(axis)
        forward = [(i, i + 1) for i in range(count - 1)]
        forward.append((count - 1, 0))
        backward = [(target, source) for source, target in forward]
        low = lax.ppermute(
            lax.slice_in_dim(block, block.shape[dim] - width, None, axis=dim), axis, forward
        )
        high = lax.ppermute(lax.slice_in_dim(block, 0, width, axis=dim), axis, backward)
        block = jnp.concatenate([low, block, high], axis=dim)
    return block


def shifted(block, axis, distance):
    devices = range(lax.axis_size(axis))
    route = [((i - distance) % len(devices), i) for i in devices]
    return lax.ppermute(block, axis, route)


def spline(squared):
    radius = jnp.sqrt(squared) * 4.0
    inner_part = 1.0 - 1.5 * radius * radius + 0.75 * radius * radius * radius
    outer_part = 0.25 * jnp.maximum(2.0 - radius, 0.0) ** 3
    return jnp.where(radius < 1.0, inner_part, outer_part) * (64.0 / 3.141592653589793)


def distance_sq(target, source_pos, offset_vec):
    squared = None
    for component in range(3):
        moved = source_pos[component] + offset_vec[component]
        gap = target[component][..., :, None] - moved[..., None, :]
        squared = gap * gap if squared is None else squared + gap * gap
    return squared


def shards(positions, masses, counts, shear_offset):
    slot_index = lax.broadcasted_iota(jnp.int32, masses.shape, 3)
    is_valid = slot_index < counts[..., None]
    weight = jnp.where(is_valid, masses, jnp.float32(0.0))
    particle_data = jnp.concatenate([positions, weight[None]], 0)
    offset = shear_offset[0]
    shear_index = lax.axis_index("shear")
    cycle_size = lax.axis_size("shear")
    cells_y = masses.shape[0]
    cells_z = masses.shape[2]
    padded = extended_2(particle_data, (("shear", 1), ("cross", 3)), 1)
    lower_row = padded[:, :1]
    upper_row = padded[:, -1:]
    lower_row = jnp.where(shear_index == 0, jnp.roll(lower_row, offset, axis=2), lower_row)
    upper_row = jnp.where(
        shear_index == cycle_size - 1, jnp.roll(upper_row, -offset, axis=2), upper_row
    )
    extended = jnp.concatenate([lower_row, padded[:, 1:-1], upper_row], 1)
    target = extended[:3, 1 : 1 + cells_y, :, 1 : 1 + cells_z]
    target_mass = extended[3, 1 : 1 + cells_y, :, 1 : 1 + cells_z]

    def source(step_y, step_z, step_x):
        picked = extended[
            :, 1 + step_y : 1 + step_y + cells_y, :, 1 + step_z : 1 + step_z + cells_z
        ]
        return jnp.roll(picked, -step_x, axis=2)

    density = jnp.zeros(masses.shape, jnp.float32)
    returned = jnp.zeros((cells_y + 2, masses.shape[1], cells_z + 2, masses.shape[3]), jnp.float32)
    half_steps = [
        (step_y, step_z, step_x)
        for step_y in (0, 1)
        for step_z in (-1, 0, 1)
        for step_x in (-1, 0, 1)
        if (step_y, step_z, step_x) >= (0, 0, 0)
    ]
    for step_y, step_z, step_x in half_steps:
        source_cells = source(step_y, step_z, step_x)
        offset_vec = (float(step_y), float(step_x), float(step_z))
        kernel = spline(distance_sq(target, source_cells[:3], offset_vec))
        density = density + jnp.sum(kernel * source_cells[3][..., None, :], axis=-1)
        if (step_y, step_z, step_x) != (0, 0, 0):
            reflected = jnp.sum(kernel * target_mass[..., :, None], axis=-2)
            reflected = jnp.roll(reflected, step_x, axis=1)
            returned = returned.at[
                1 + step_y : 1 + step_y + cells_y, :, 1 + step_z : 1 + step_z + cells_z
            ].add(reflected)
    from_below = shifted(returned[:, :, cells_z + 1], "cross", 1)
    from_above = shifted(returned[:, :, 0], "cross", -1)
    returned = returned.at[:, :, 1].add(from_below)
    returned = returned.at[:, :, cells_z].add(from_above)
    top_row = returned[cells_y + 1, :, 1 : 1 + cells_z]
    arrived = shifted(top_row, "shear", 1)
    arrived = jnp.where(shear_index == 0, jnp.roll(arrived, offset, axis=0), arrived)
    owned = returned[1 : 1 + cells_y, :, 1 : 1 + cells_z].at[0].add(arrived)
    density = density + owned
    return jnp.where(is_valid, density, jnp.float32(0.0))


def solution(mesh):
    in_specs = (
        P(None, "shear", None, "cross", None),
        P("shear", None, "cross", None),
        P("shear", None, "cross"),
        P(),
    )
    out_specs = P("shear", None, "cross", None)
    return jax.shard_map(shards, mesh=mesh, in_specs=in_specs, out_specs=out_specs, check_vma=False)
```

profile of v0, /device:TPU:0, one launch (start us, length us, event | category | flops | bytes accessed | tf_op | source)
XLA Modules:
  0.0 106.2 jit_solution(14543194713814763750)
XLA Ops:
  0.0 0.8 constant_dynamic-update-slice_fusion
  0.8 0.8 multiply_bitcast_fusion
  1.6 7.0 %collective-permute-start.1 = (f32[4,1,16,1,256]{4,3,2,1,0:T(1,128)S(1)}, f32[4,1,16,1,256]{4,3,2,1,0:T(1,128)S(1)}, u32[]{:S(2)}, u32[]{:S(2)}) collective-permute-start(f32[4,1,16,1,256]{4,3,2,1,0:T(1,128)S(1)} %copy_dynamic-update-slice_fusion), channel_id=1, source_target_pairs={{2,0},{4,2},{6,4},{8,6},{10,8},{12,10},{14,12},{16,14},{18,16},{20... | collective-permute-start | bytes 196616 | tf_op jit(solution)/shard_map/ppermute | solution.py:16
  8.6 0.8 fusion.127
  10.2 0.3 collective-permute-done.1
  10.5 6.0 %collective-permute-done = f32[4,1,16,1,256]{4,3,2,1,0:T(1,128)S(1)} collective-permute-done((f32[4,1,16,1,256]{4,3,2,1,0:T(1,128)S(1)}, f32[4,1,16,1,256]{4,3,2,1,0:T(1,128)S(1)}, u32[]{:S(2)}, u32[]{:S(2)}) %collective-permute-start) | collective-permute-done | bytes 65568 | tf_op jit(solution)/shard_map/ppermute | solution.py:13
  16.5 0.2 pad_maximum_fusion.4
  16.8 0.5 collective-permute-start.2
  17.3 0.9 collective-permute-done.3
  18.2 0.3 collective-permute-done.2
  18.7 0.2 fusion.45
  18.9 0.2 slice_add_fusion.6
  19.1 0.2 fusion.123
  19.8 20.8 %multiply_reduce_fusion.13 = (f32[16,256]{1,0:T(8,128)S(1)}, f32[16,256]{1,0:T(8,128)S(1)}, f32[16,256]{1,0:T(8,128)S(1)}, f32[16,256]{1,0:T(8,128)S(1)}, f32[16...) fusion(f32[16,256]{1,0:T(8,128)S(1)} %bitcast.261, f32[16,256]{1,0:T(8,128)S(1)} %bitcast.258, ...), kind=kLoop, calls=%fused_computation.85 | loop fusion | flops 111120384 | bytes 376832 | tf_op jit(solution)/shard_map/reduce_sum | solution.py:83
  40.9 16.2 %multiply_reduce_fusion.15 = (f32[16,256]{1,0:T(8,128)S(1)}, f32[16,256]{1,0:T(8,128)S(1)}, f32[16,256]{1,0:T(8,128)S(1)}, f32[16,256]{1,0:T(8,128)S(1)}, f32[16,256]{1,0:T(8,128)S(1)}, /*index=5*/f32[16,256]{1,0:T(8,128)S(1)}) fusion(f32[16,256]{1,0:T(8,128)S(1)} %bitcast.240, f32[16,256]{1,0:T(8,128)S(1)} %bitcast.244, ...), kind=kLoop, calls=%fused_computation.89 | loop fusion | flops 84910080 | bytes 360448 | tf_op jit(solution)/shard_map/reduce_sum | solution.py:83
  57.5 16.2 %multiply_reduce_fusion.16 = (f32[16,256]{1,0:T(8,128)S(1)}, f32[16,256]{1,0:T(8,128)S(1)}, f32[16,256]{1,0:T(8,128)S(1)}, f32[16,256]{1,0:T(8,128)S(1)}, f32[16,256]{1,0:T(8,128)S(1)}, /*index=5*/f32[16,256]{1,0:T(8,128)S(1)}) fusion(f32[16,256]{1,0:T(8,128)S(1)} %bitcast.267, f32[16,256]{1,0:T(8,128)S(1)} %bitcast.266, ...), kind=kLoop, calls=%fused_computation.91 | loop fusion | flops 84910080 | bytes 360448 | tf_op jit(solution)/shard_map/reduce_sum | solution.py:83
  73.9 16.2 %multiply_reduce_fusion.14 = (f32[16,256]{1,0:T(8,128)S(1)}, f32[16,256]{1,0:T(8,128)S(1)}, f32[16,256]{1,0:T(8,128)S(1)}, f32[16,256]{1,0:T(8,128)S(1)}, f32[16,256]{1,0:T(8,128)S(1)}, /*index=5*/f32[16,256]{1,0:T(8,128)S(1)}) fusion(f32[16,256]{1,0:T(8,128)S(1)} %get-tuple-element.343, f32[16,256]{1,0:T(8,128)S(1)} %get-tuple-element.344, ...), kind=kLoop, calls=%fused_computation.87 | loop fusion | flops 84910080 | bytes 360448 | tf_op jit(solution)/shard_map/reduce_sum | solution.py:83
  90.3 6.2 %multiply_reduce_fusion.17 = (f32[16,256]{1,0:T(8,128)S(1)}, f32[16,256]{1,0:T(8,128)S(1)}) fusion(f32[16,256]{1,0:T(8,128)S(1)} %get-tuple-element.347, f32[16,256]{1,0:T(8,128)S(1)} %get-tuple-element.348, f32[16,256]{1,0:T(8,128)S(1)} %get-tuple-element.333, f32[16,256]{1,0:T(8,128)S(1)} %get-tuple-element.349, f32[16,256]{1,0:T(8,128)S(1)} %get-tuple-element.334, ...), kind=kLoop, calls=%fused_computation.93 | loop fusion | flops 28303360 | bytes 163840 | tf_op jit(solution)/shard_map/reduce_sum | solution.py:83
  96.6 0.3 collective-permute-start.4
  96.9 0.3 collective-permute-start.5
  97.2 0.7 collective-permute-done.4
  97.9 0.2 collective-permute-done.5
  98.2 7.3 %collective-permute-done.6 = f32[16,1,256]{2,0,1:T(8,128)S(1)} collective-permute-done((f32[16,1,256]{2,0,1:T(8,128)S(1)}, f32[16,1,256]{2,0,1:T(8,128)S(1)}, u32[]{:S(2)}, u32[]{:S(2)}) %collective-permute-start.6) | collective-permute-done | bytes 16416 | tf_op jit(solution)/shard_map/ppermute | solution.py:24
  105.6 0.6 copy.9
  (92 shorter events, 1.6 us)
Async XLA Ops:
  1.6 8.9 %collective-permute-start.1 = (f32[4,1,16,1,256]{4,3,2,1,0:T(1,128)S(1)}, f32[4,1,16,1,256]{4,3,2,1,0:T(1,128)S(1)}, u32[]{:S(2)}, u32[]{:S(2)}) collective-permute-start(f32[4,1,16,1,256]{4,3,2,1,0:T(1,128)S(1)} %copy_dynamic-update-slice_fusion), channel_id=1, source_target_pairs={{2,0},{4,2},{6,4},{8,6},{10,8},{12,10},{14,12},{16,14},{18,16},{20... | collective-permute-start | bytes 196616 | tf_op jit(solution)/shard_map/ppermute | solution.py:16
  8.6 7.9 %collective-permute-start = (f32[4,1,16,1,256]{4,3,2,1,0:T(1,128)S(1)}, f32[4,1,16,1,256]{4,3,2,1,0:T(1,128)S(1)}, u32[]{:S(2)}, u32[]{:S(2)}) collective-permute-start(f32[4,1,16,1,256]{4,3,2,1,0:T(1,128)S(1)} %copy_dynamic-update-slice_fusion), channel_id=1, source_target_pairs={{0,2},{2,4},{4,6},{6,8},{8,10},{10,12},{12,14},{14,16},{16,18},{18... | collective-permute-start | bytes 196616 | tf_op jit(solution)/shard_map/ppermute | solution.py:13
  16.7 1.5 %collective-permute-start.3 = (f32[4,3,16,1,256]{4,3,2,1,0:T(1,128)S(1)}, f32[4,3,16,1,256]{4,3,2,1,0:T(1,128)S(1)}, u32[]{:S(2)}, u32[]{:S(2)}) collective-permute-start(f32[4,3,16,1,256]{4,3,2,1,0:T(1,128)S(1)} %pad_maximum_fusion.4), channel_id=1, source_target_pairs={{0,1},{1,0},{2,3},{3,2},{4,5},{5,4},{6,7},{7,6},{8,9},{9,8},{10,11... | collective-permute-start | bytes 589832 | tf_op jit(solution)/shard_map/ppermute | solution.py:13
  16.8 1.7 %collective-permute-start.2 = (f32[4,3,16,1,256]{4,3,2,1,0:T(1,128)S(1)}, f32[4,3,16,1,256]{4,3,2,1,0:T(1,128)S(1)}, u32[]{:S(2)}, u32[]{:S(2)}) collective-permute-start(f32[4,3,16,1,256]{4,3,2,1,0:T(1,128)S(1)} %pad_maximum_fusion.4), channel_id=1, source_target_pairs={{1,0},{0,1},{3,2},{2,3},{5,4},{4,5},{7,6},{6,7},{9,8},{8,9},{11,10... | collective-permute-start | bytes 589832 | tf_op jit(solution)/shard_map/ppermute | solution.py:16
  96.5 9.0 %copy-start = (s32[1,16,1]{1,2,0:T(1,128)S(1)}, s32[1,16,1]{1,2,0:T(1,128)}, u32[]{:S(2)}) copy-start(s32[1,16,1]{1,2,0:T(1,128)} %param.38) | copy-start | bytes 196
  96.6 1.3 %collective-permute-start.4 = (f32[3,16,256]{2,1,0:T(8,128)S(1)}, f32[3,16,256]{2,1,0:T(8,128)S(1)}, u32[]{:S(2)}, u32[]{:S(2)}) collective-permute-start(f32[3,16,256]{2,1,0:T(8,128)S(1)} %get-tuple-element.278), channel_id=1, source_target_pairs={{1,0},{0,1},{3,2},{2,3},{5,4},{4,5},{7,6},{6,7},{9,8},{8,9},{11,10... | collective-permute-start | bytes 147464 | tf_op jit(solution)/shard_map/ppermute | solution.py:24
  96.9 1.2 %collective-permute-start.5 = (f32[3,16,256]{2,1,0:T(8,128)S(1)}, f32[3,16,256]{2,1,0:T(8,128)S(1)}, u32[]{:S(2)}, u32[]{:S(2)}) collective-permute-start(f32[3,16,256]{2,1,0:T(8,128)S(1)} %get-tuple-element.279), channel_id=1, source_target_pairs={{1,0},{0,1},{3,2},{2,3},{5,4},{4,5},{7,6},{6,7},{9,8},{8,9},{11,10... | collective-permute-start | bytes 147464 | tf_op jit(solution)/shard_map/ppermute | solution.py:24
  98.1 7.4 %collective-permute-start.6 = (f32[16,1,256]{2,0,1:T(8,128)S(1)}, f32[16,1,256]{2,0,1:T(8,128)S(1)}, u32[]{:S(2)}, u32[]{:S(2)}) collective-permute-start(f32[16,1,256]{2,0,1:T(8,128)S(1)} %slice_bitcast_fusion.2), channel_id=1, source_target_pairs={{30,0},{0,2},{2,4},{4,6},{6,8},{8,10},{10,12},{12,14},{14,16},{16,... | collective-permute-start | bytes 49160 | tf_op jit(solution)/shard_map/ppermute | solution.py:24
where the time goes:
time: 107 us; the launch traced here: 106 us
  other arithmetic  78.1 us (73%)
  waiting for transfers between devices  15.7 us (15%)
  starting transfers between devices  8.22 us (8%)
  local copies, waits for them, and re-layouts  2.73 us (3%)
  between operations  1.44 us (1%)
    reduce_sum x5, other arithmetic, shards(): density = density + jnp.sum(kernel * source_cells[3][..., None, :], axis=-1)  75.6 us
    ppermute x3, waiting for transfers between devices, shifted(): return lax.ppermute(block, axis, route)  8.24 us
    ppermute x2, starting transfers between devices, extended_2(): lax.ppermute(lax.slice_in_dim(block, 0, width, axis=dim), axis, backward)  7.51 us
    ppermute x2, waiting for transfers between devices, extended_2(): lax.ppermute(lax.slice_in_dim(block, block.shape[dim] - width, None, axis...  6.88 us
  transfers between devices with their start and end apart: 7, of which 7 were waited for; matrix products, arithmetic and copies ran while one was open for 1% of the time, Pallas kernels for 0%

commit v1 on v0

v1 whole, which is shorter than its diff:
```python
import functools
import jax
import jax.numpy as jnp
from jax import lax
from jax.experimental import pallas as pl
from jax.experimental.pallas import tpu as pltpu
from jax.sharding import PartitionSpec as P

BLOCK = 16
PER_CHUNK = 8
FEATURES = 32


def extended_2(block, sides, width):
    for axis, dim in sides:
        count = lax.axis_size(axis)
        forward = [(i, (i + 1) % count) for i in range(count)]
        backward = [(target, source) for source, target in forward]
        low = lax.ppermute(
            lax.slice_in_dim(block, block.shape[dim] - width, None, axis=dim), axis, forward
        )
        high = lax.ppermute(lax.slice_in_dim(block, 0, width, axis=dim), axis, backward)
        block = jnp.concatenate([low, block, high], axis=dim)
    return block


def split3(x):
    high = lax.reduce_precision(x, 8, 7)
    rest = x - high
    middle = lax.reduce_precision(rest, 8, 7)
    low = lax.reduce_precision(rest - middle, 8, 7)
    return high, middle, low


def source_rows(coords, weight):
    rows = []
    for value in coords:
        high, middle, low = split3(value)
        rows += [high, high, high, middle, middle, low]
    norm = coords[0] * coords[0] + coords[1] * coords[1] + coords[2] * coords[2]
    one = jnp.ones_like(norm)
    zero = jnp.zeros_like(norm)
    rows += list(split3(norm)) + [one] * 3 + list(split3(weight))
    rows += [zero] * (FEATURES - len(rows))
    return jnp.stack(rows, axis=-2).astype(jnp.bfloat16)


def target_rows(coords):
    rows = []
    for value in coords:
        high, middle, low = split3(-2.0 * value)
        rows += [high, middle, low, high, middle, high]
    norm = coords[0] * coords[0] + coords[1] * coords[1] + coords[2] * coords[2]
    one = jnp.ones_like(norm)
    zero = jnp.zeros_like(norm)
    rows += [one] * 3 + list(split3(norm))
    rows += [zero] * (FEATURES - len(rows))
    return jnp.stack(rows, axis=-2).astype(jnp.bfloat16)


def density_kernel(
    rooms, list_ref, chunks_ref, counts_ref, pos_ref, feat_ref, target_ref, out_ref,
    store_ref, lhs_a, lhs_b, sq_a, sq_b,
):
    cells, slots = out_ref.shape
    pairs = pos_ref.shape[0]
    unroll = 4
    zero_block = pairs * 2 * rooms
    store_ref[zero_block] = jnp.zeros((BLOCK, 128), jnp.bfloat16)
    row_id = lax.broadcasted_iota(jnp.int32, (rooms * BLOCK, slots), 0)

    def compact(step, carry):
        for k in range(unroll):
            pair = step * unroll + k
            chosen = jnp.where(row_id == pos_ref[pair], 1.0, 0.0).astype(jnp.bfloat16)
            for variant in range(2):
                rows = lax.dot_general(
                    chosen, feat_ref[pair, variant], (((1,), (1,)), ((), ())),
                    preferred_element_type=jnp.float32,
                )
                rows = jnp.concatenate(
                    [rows, jnp.zeros((rooms * BLOCK, 128 - FEATURES), jnp.float32)], axis=1
                )
                store_ref[pl.ds((pair * 2 + variant) * rooms, rooms)] = rows.astype(
                    jnp.bfloat16
                ).reshape(rooms, BLOCK, 128)
        return carry

    lax.fori_loop(0, pairs // unroll, compact, 0)

    mass_rows = lax.broadcasted_iota(jnp.int32, (FEATURES, 128), 0)
    spread = jnp.where((mass_rows >= 24) & (mass_rows < 27), 1.0, 0.0).astype(jnp.bfloat16)
    pad = jnp.zeros((128 - FEATURES, slots + 128), jnp.bfloat16)

    def cell_body(cell, carry):
        weights = jnp.concatenate([target_ref[cell], spread], axis=1)
        weights = jnp.concatenate([weights, pad], axis=0)

        def produce(chunk, sq_ref):
            blocks = [
                store_ref[list_ref[cell, chunk * PER_CHUNK + k]] for k in range(PER_CHUNK)
            ]
            lhs = jnp.concatenate(blocks, axis=0)
            sq_ref[...] = jnp.dot(lhs, weights, preferred_element_type=jnp.float32)

        def consume(sq_ref, acc):
            for group in range(PER_CHUNK * BLOCK // 8):
                rows = pl.ds(group * 8, 8)
                squared = jnp.maximum(sq_ref[rows, :slots], 1e-30)
                mass = sq_ref[rows, slots:]
                mass = jnp.concatenate([mass] * (slots // 128), axis=1)
                q = squared * lax.rsqrt(squared)
                outer = jnp.maximum(2.0 - q, 0.0)
                inner = jnp.maximum(outer - 1.0, 0.0)
                value = outer * outer * outer - 4.0 * (inner * inner * inner)
                acc = acc + mass * value
            return acc

        produce(0, sq_a)

        def pair_body(step, acc):
            produce(2 * step + 1, sq_b)
            acc = consume(sq_a, acc)
            produce(2 * step + 2, sq_a)
            return consume(sq_b, acc)

        acc = lax.fori_loop(
            0, (chunks_ref[cell] + 1) // 2, pair_body, jnp.zeros((8, slots), jnp.float32)
        )
        total = jnp.sum(acc, axis=0, keepdims=True) * (16.0 / 3.141592653589793)
        slot = lax.broadcasted_iota(jnp.int32, (1, slots), 1)
        out_ref[pl.ds(cell, 1), :] = jnp.where(slot < counts_ref[cell], total, 0.0)
        return carry

    lax.fori_loop(0, cells, cell_body, 0)


def shards(positions, masses, counts, shear_offset):
    cells_y, cells, cells_z, slots = masses.shape
    assert cells_y == 1 and cells_z == 1
    rooms = slots // BLOCK + 1
    slot_index = lax.broadcasted_iota(jnp.int32, masses.shape, 3)
    weight = jnp.where(slot_index < counts[..., None], masses, jnp.float32(0.0))
    data = jnp.concatenate([positions, weight[None]], 0)
    offset = shear_offset[0]
    shear_index = lax.axis_index("shear")
    cycle = lax.axis_size("shear")
    padded = extended_2(data, (("shear", 1), ("cross", 3)), 1)
    low_shift = jnp.where(shear_index == 0, -offset, 0)
    high_shift = jnp.where(shear_index == cycle - 1, offset, 0)

    features, masks, shifts = [], [], []
    for step_y in (-1, 0, 1):
        for step_z in (-1, 0, 1):
            y, x, z, mass = (padded[k, 1 + step_y, :, 1 + step_z] for k in range(4))
            keep = mass > 0.0
            for value, step in ((y, step_y), (z, step_z)):
                if step == -1:
                    keep = keep & (value >= 0.5)
                elif step == 1:
                    keep = keep & (value <= 0.5)
            lower = x <= 0.5
            masks.append(jnp.stack([keep & lower, keep & ~lower], 0))
            moved = jnp.where(lower, x + 1.0, x - 1.0)
            scaled_y = 4.0 * (y + (step_y - 0.5))
            scaled_z = 4.0 * (z + (step_z - 0.5))
            features.append(
                jnp.stack(
                    [
                        source_rows((scaled_y, 4.0 * (value - 0.5), scaled_z), mass)
                        for value in (x, moved)
                    ],
                    1,
                )
            )
            shifts.append({-1: low_shift, 0: jnp.int32(0), 1: high_shift}[step_y])
    features = jnp.concatenate(features, 0)
    chosen = jnp.stack(masks, 0)
    triangle = (
        lax.broadcasted_iota(jnp.int32, (slots, slots), 0)
        <= lax.broadcasted_iota(jnp.int32, (slots, slots), 1)
    ).astype(jnp.bfloat16)
    ranks = jnp.dot(
        chosen.reshape(-1, slots).astype(jnp.bfloat16), triangle,
        preferred_element_type=jnp.float32,
    ).astype(jnp.int32).reshape(chosen.shape)
    sizes = ranks[..., -1]
    blocks = (sizes + (BLOCK - 1)) // BLOCK
    pos = jnp.where(
        chosen[:, 0],
        ranks[:, 0] - 1,
        jnp.where(chosen[:, 1], ranks[:, 1] - 1 + BLOCK * blocks[:, 0, :, None], -1),
    ).reshape(-1, 1, slots)

    relations = len(masks)
    shift = jnp.stack(shifts)
    target = lax.broadcasted_iota(jnp.int32, (cells, relations, 3), 0)
    relation = lax.broadcasted_iota(jnp.int32, (cells, relations, 3), 1)
    step_x = lax.broadcasted_iota(jnp.int32, (cells, relations, 3), 2) - 1
    cell = (target + step_x + shift[None, :, None] + 2 * cells) % cells
    match = cell[..., None] == jnp.arange(cells, dtype=jnp.int32)
    first = jnp.sum(jnp.where(match, blocks[None, :, 0, None, :], 0), -1)
    second = jnp.sum(jnp.where(match, blocks[None, :, 1, None, :], 0), -1)
    length = jnp.where(step_x == 0, first + second, jnp.where(step_x < 0, second, first))
    variant = jnp.where(step_x == 0, 0, 1)
    start = ((relation * cells + cell) * 2 + variant) * rooms + jnp.where(step_x < 0, first, 0)
    length = length.reshape(cells, -1)
    start = start.reshape(cells, -1)
    end = jnp.cumsum(length, axis=1)
    begin = end - length
    room = relations * 3 * rooms + 3 * PER_CHUNK
    room = (room + 127) // 128 * 128
    index = lax.broadcasted_iota(jnp.int32, (cells, relations * 3, room), 2)
    inside = (index >= begin[..., None]) & (index < end[..., None])
    zero_block = relations * cells * 2 * rooms
    block_list = zero_block + jnp.sum(
        jnp.where(inside, (start - begin)[..., None] + index - zero_block, 0), 1
    )
    chunks = (end[:, -1] + (PER_CHUNK - 1)) // PER_CHUNK

    own = padded[:3, 1, :, 1]
    targets = target_rows(tuple(4.0 * (own[k] - 0.5) for k in range(3)))

    smem = pl.BlockSpec(memory_space=pltpu.SMEM)
    vmem = pl.BlockSpec(memory_space=pltpu.VMEM)
    rows = PER_CHUNK * BLOCK
    density = pl.pallas_call(
        functools.partial(density_kernel, rooms),
        out_shape=jax.ShapeDtypeStruct((cells, slots), jnp.float32),
        in_specs=[smem, smem, smem, vmem, vmem, vmem],
        out_specs=vmem,
        scratch_shapes=[
            pltpu.VMEM((relations * cells * 2 * rooms + 1, BLOCK, 128), jnp.bfloat16),
            pltpu.VMEM((rows, 128), jnp.bfloat16),
            pltpu.VMEM((rows, 128), jnp.bfloat16),
            pltpu.VMEM((rows, slots + 128), jnp.float32),
            pltpu.VMEM((rows, slots + 128), jnp.float32),
        ],
        compiler_params=pltpu.CompilerParams(vmem_limit_bytes=56 * 1024 * 1024),
        name="density",
    )(block_list, chunks, counts.reshape(-1), pos, features, targets)
    return density.reshape(masses.shape)


def solution(mesh):
    in_specs = (
        P(None, "shear", None, "cross", None),
        P("shear", None, "cross", None),
        P("shear", None, "cross"),
        P(),
    )
    out_specs = P("shear", None, "cross", None)
    return jax.shard_map(shards, mesh=mesh, in_specs=in_specs, out_specs=out_specs, check_vma=False)
```

time: 107 us -> 95.8 us (0.90)
  other arithmetic: 78.1 us -> 29.5 us
  Pallas kernels: 0 us -> 42.5 us
  waiting for transfers between devices: 15.7 us -> 0.8 us
  local copies, waits for them, and re-layouts: 2.73 us -> 11.6 us
  between operations: 1.44 us -> 2.65 us
    reduce_sum x5 -> x2, other arithmetic: 75.6 us -> 1.39 us  [the longest x1 1.12 us: shards(): first = jnp.sum(jnp.where(match, blocks[None, :, 0, None, :], 0), -1)]
    pallas_call x0 -> x1, Pallas kernels: none -> 42.5 us  [shards(): pl.pallas_call(functools.partial(density_kernel, rooms), out_shape=jax.Sh...]
    unnamed x0 -> x16, other arithmetic: none -> 19.2 us
    ppermute x3 -> x0, waiting for transfers between devices: 8.24 us -> none  [shifted(): return lax.ppermute(block, axis, route)]
    ppermute x2, waiting for transfers between devices: 6.88 us -> 0.7 us  [extended_2(): lax.ppermute(lax.slice_in_dim(block, block.shape[dim] - width, None, axis...]
    another operation x0 -> x179, local copies, waits for them, and re-layouts: none -> 5.78 us  [the longest x2 3.15 us: target_rows(): return jnp.stack(rows, axis=-2).astype(jnp.bfloat16)]
    unnamed x47 -> x8, local copies, waits for them, and re-layouts: 0.96 us -> 3.42 us
    concatenate x1 -> x2, other arithmetic: 0.01 us -> 2.36 us  [the longest x1 2.36 us: shards(): features = jnp.concatenate(features, 0)]
  transfers between devices with their start and end apart: 7 -> 4, of which waited for: 7 -> 2; matrix products, arithmetic and copies ran while one was open for 1% -> 7% of each run, Pallas kernels for 0% -> 0%
where the time goes in v1:
time: 95.8 us; the launch traced here: 94.9 us
  Pallas kernels  42.5 us (44%)
  other arithmetic  29.5 us (31%)
  local copies, waits for them, and re-layouts  11.6 us (12%)
  starting transfers between devices  7.58 us (8%)
  between operations  2.65 us (3%)
    pallas_call x1, Pallas kernels, shards(): pl.pallas_call(functools.partial(density_kernel, rooms), out_shape=jax.Sh...  42.5 us
    unnamed x16, other arithmetic  19.2 us
    ppermute x2, starting transfers between devices, extended_2(): lax.ppermute(lax.slice_in_dim(block, 0, width, axis=dim), axis, backward)  7.51 us
    unnamed x8, local copies, waits for them, and re-layouts  3.42 us
    another operation x2, local copies, waits for them, and re-layouts, target_rows(): return jnp.stack(rows, axis=-2).astype(jnp.bfloat16)  3.15 us
    concatenate x1, other arithmetic, shards(): features = jnp.concatenate(features, 0)  2.36 us
  transfers between devices with their start and end apart: 4, of which 2 were waited for; matrix products, arithmetic and copies ran while one was open for 7% of the time, Pallas kernels for 0%

profile of v1, /device:TPU:0, one launch (start us, length us, event | category | flops | bytes accessed | tf_op | source)
XLA Modules:
  0.0 94.9 jit_solution(8872046244037538599)
XLA Ops:
  0.0 0.8 copy.2200
  0.8 0.8 fusion.455
  1.6 7.0 %collective-permute-start.1 = (f32[4,1,16,1,256]{4,2,3,1,0:T(8,128)S(1)}, f32[4,1,16,1,256]{4,2,3,1,0:T(8,128)S(1)}, u32[]{:S(2)}, u32[]{:S(2)}) collective-permute-start(f32[4,1,16,1,256]{4,2,3,1,0:T(8,128)S(1)} %pad_maximum_fusion.73), channel_id=1, source_target_pairs={{2,0},{4,2},{6,4},{8,6},{10,8},{12,10},{14,12},{16,14},{18,16},{20... | collective-permute-start | bytes 196616 | tf_op jit(solution)/shard_map/ppermute | solution.py:22
  8.7 0.8 fusion.407
  9.5 0.8 bitcast_and_fusion.4
  12.6 3.1 %stack.1276.target_ref = bf16[16,32,256]{2,1,0:T(8,128)(2,1)} concatenate(bf16[16,1,256]{2,1,0:T(2,128)(2,1)S(1)} %copy.2730, bf16[16,1,256]{2,1,0:T(2,128)(2,1)S(1)} %copy.2731, bf16[16,1,256]{2,1,0:T(2,128)(2,1)S(1)} %copy.2732, bf16[16,1,256]{2,1,0:T(2,128)(2,1)S(1)} %copy.2730, bf16[16,1,256]{2,1,0:T(2,128)(2,1)S(1)} %copy.2731, bf16[16,1,256]{2,1,0:T(2,128)(2,1)S(1)} %copy.2730, ...), dimensions={1} | concatenate | bytes 524288 | tf_op jit(solution)/shard_map/stack | solution.py:58
  15.8 0.7 collective-permute-done
  16.6 0.5 collective-permute-start.3
  19.3 1.1 %select_reduce_fusion.2 = (s32[16,9,3]{0,2,1:T(4,128)S(1)}, s32[16,9,3]{0,2,1:T(4,128)S(1)}) fusion(s32[9,16]{1,0:T(8,128)S(1)} %bitcast.1295, s32[16,9,3]{0,2,1:T(4,128)S(1)} %add_select_fusion, s32[9,16]{1,0:T(8,128)S(1)} %bitcast.1296), kind=kLoop, calls=%fused_computation.153 | loop fusion | flops 33696 | bytes 6336 | tf_op jit(solution)/shard_map/reduce_sum | solution.py:202
  21.6 0.6 broadcast_add_fusion.list_ref
  22.2 0.5 and_select_fusion.1.chunks_ref
  26.2 1.1 %copy_select_fusion.pos_ref = s32[144,1,256]{2,1,0:T(1,128)} fusion(pred[144,1,256]{2,0,1:T(8,128)(4,1)S(1)} %bitcast.1291, pred[144,1,256]{2,0,1:T(8,128)(4,1)S(1)} %bitcast.1290, s32[9,1,16,256]{3,1,2,0:T(1,128)S(1)} %copy.2759, s32[9,1,16,256]{3,1,2,0:T(1,128)S(1)} %copy.2758, s32[144]{0:T(256)S(1)} %mul.5666), kind=kLoop, calls=%fused_computation.77 | loop fusion | flops 110592 | bytes 516672 | tf_op jit(solution)/shard_map/jit(_where)/select_n | solution.py:189
  27.4 2.6 %fusion.29 = bf16[144,2,32,256]{3,2,1,0:T(8,128)(2,1)S(1)} fusion(bf16[16,1,4,256]{3,2,1,0:T(4,128)(2,1)S(1)} %stack.529, bf16[16,1,1,256]{3,2,1,0:T(2,128)(2,1)S(1)} %stack.528, bf16[16,1,1,256]{3,2,1,0:T(2,128)(2,1)S(1)} %copy.2246, bf16[16,1,2,256]{3,2,1,0:T(2,128)(2,1)S(1)} %stack.524, bf16[16,1,1,256]{3,2,1,0:T(2,128)(2,1)S(1)} %stack.523, ...), kind=kLoop, calls=%fused_computation.107 | loop fusion | flops 29360128 | bytes 761856
  30.0 2.4 %fusion.31 = bf16[144,2,32,256]{3,2,1,0:T(8,128)(2,1)S(1)} fusion(bf16[144,2,32,256]{3,2,1,0:T(8,128)(2,1)S(1)} %fusion.29, bf16[16,1,4,256]{3,2,1,0:T(4,128)(2,1)S(1)} %stack.529, bf16[16,1,1,256]{3,2,1,0:T(2,128)(2,1)S(1)} %stack.528, bf16[16,1,1,256]{3,2,1,0:T(2,128)(2,1)S(1)} %copy.2303, bf16[16,1,2,256]{3,2,1,0:T(2,128)(2,1)S(1)} %stack.524, ...), kind=kLoop, calls=%fused_computation.109 | loop fusion | flops 29360128 | bytes 950272
  32.4 2.4 %fusion.33 = bf16[144,2,32,256]{3,2,1,0:T(8,128)(2,1)S(1)} fusion(bf16[144,2,32,256]{3,2,1,0:T(8,128)(2,1)S(1)} %fusion.31, bf16[16,1,4,256]{3,2,1,0:T(4,128)(2,1)S(1)} %stack.529, bf16[16,1,1,256]{3,2,1,0:T(2,128)(2,1)S(1)} %stack.528, bf16[16,1,1,256]{3,2,1,0:T(2,128)(2,1)S(1)} %copy.2359, bf16[16,1,2,256]{3,2,1,0:T(2,128)(2,1)S(1)} %stack.524, ...), kind=kLoop, calls=%fused_computation.111 | loop fusion | flops 29360128 | bytes 950272
  34.7 2.4 %fusion.35 = bf16[144,2,32,256]{3,2,1,0:T(8,128)(2,1)S(1)} fusion(bf16[144,2,32,256]{3,2,1,0:T(8,128)(2,1)S(1)} %fusion.33, bf16[16,1,4,256]{3,2,1,0:T(4,128)(2,1)S(1)} %stack.529, bf16[16,1,1,256]{3,2,1,0:T(2,128)(2,1)S(1)} %stack.528, bf16[16,1,1,256]{3,2,1,0:T(2,128)(2,1)S(1)} %copy.2416, bf16[16,1,2,256]{3,2,1,0:T(2,128)(2,1)S(1)} %stack.524, ...), kind=kLoop, calls=%fused_computation.113 | loop fusion | flops 29360128 | bytes 950272
  37.1 2.4 %fusion.37 = bf16[144,2,32,256]{3,2,1,0:T(8,128)(2,1)S(1)} fusion(bf16[144,2,32,256]{3,2,1,0:T(8,128)(2,1)S(1)} %fusion.35, bf16[16,1,4,256]{3,2,1,0:T(4,128)(2,1)S(1)} %stack.529, bf16[16,1,1,256]{3,2,1,0:T(2,128)(2,1)S(1)} %stack.528, bf16[16,1,1,256]{3,2,1,0:T(2,128)(2,1)S(1)} %copy.2478, bf16[16,1,2,256]{3,2,1,0:T(2,128)(2,1)S(1)} %stack.524, ...), kind=kLoop, calls=%fused_computation.115 | loop fusion | flops 29360128 | bytes 950272
  39.4 2.4 %fusion.39 = bf16[144,2,32,256]{3,2,1,0:T(8,128)(2,1)S(1)} fusion(bf16[144,2,32,256]{3,2,1,0:T(8,128)(2,1)S(1)} %fusion.37, bf16[16,1,4,256]{3,2,1,0:T(4,128)(2,1)S(1)} %stack.529, bf16[16,1,1,256]{3,2,1,0:T(2,128)(2,1)S(1)} %stack.528, bf16[16,1,1,256]{3,2,1,0:T(2,128)(2,1)S(1)} %copy.2535, bf16[16,1,2,256]{3,2,1,0:T(2,128)(2,1)S(1)} %stack.524, ...), kind=kLoop, calls=%fused_computation.117 | loop fusion | flops 29360128 | bytes 950272
  41.8 2.4 %fusion.41 = bf16[144,2,32,256]{3,2,1,0:T(8,128)(2,1)S(1)} fusion(bf16[144,2,32,256]{3,2,1,0:T(8,128)(2,1)S(1)} %fusion.39, bf16[16,1,4,256]{3,2,1,0:T(4,128)(2,1)S(1)} %stack.529, bf16[16,1,1,256]{3,2,1,0:T(2,128)(2,1)S(1)} %stack.528, bf16[16,1,1,256]{3,2,1,0:T(2,128)(2,1)S(1)} %copy.2591, bf16[16,1,2,256]{3,2,1,0:T(2,128)(2,1)S(1)} %stack.524, ...), kind=kLoop, calls=%fused_computation.119 | loop fusion | flops 29360128 | bytes 950272
  44.2 2.4 %fusion.43 = bf16[144,2,32,256]{3,2,1,0:T(8,128)(2,1)S(1)} fusion(bf16[144,2,32,256]{3,2,1,0:T(8,128)(2,1)S(1)} %fusion.41, bf16[16,1,4,256]{3,2,1,0:T(4,128)(2,1)S(1)} %stack.529, bf16[16,1,1,256]{3,2,1,0:T(2,128)(2,1)S(1)} %stack.528, bf16[16,1,1,256]{3,2,1,0:T(2,128)(2,1)S(1)} %copy.2649, bf16[16,1,2,256]{3,2,1,0:T(2,128)(2,1)S(1)} %stack.524, ...), kind=kLoop, calls=%fused_computation.121 | loop fusion | flops 29360128 | bytes 950272
  46.5 2.4 %fusion.45.feat_ref = bf16[144,2,32,256]{3,2,1,0:T(8,128)(2,1)S(1)} fusion(bf16[144,2,32,256]{3,2,1,0:T(8,128)(2,1)S(1)} %fusion.43, bf16[16,1,4,256]{3,2,1,0:T(4,128)(2,1)S(1)} %stack.529, bf16[16,1,1,256]{3,2,1,0:T(2,128)(2,1)S(1)} %stack.528, bf16[16,1,1,256]{3,2,1,0:T(2,128)(2,1)S(1)} %copy.2704, bf16[16,1,2,256]{3,2,1,0:T(2,128)(2,1)S(1)} %stack.524, ...), kind=kLoop, calls=%fused_computation.123 | loop fusion | flops 29360128 | bytes 950272 | tf_op jit(solution)/shard_map/concatenate | solution.py:177
  48.9 2.1 %copy-done = bf16[144,2,32,256]{3,2,1,0:T(8,128)(2,1)} copy-done((bf16[144,2,32,256]{3,2,1,0:T(8,128)(2,1)}, bf16[144,2,32,256]{3,2,1,0:T(8,128)(2,1)S(1)}, u32[]{:S(2)}) %copy-start) | copy-done | bytes 4718616
  51.1 42.5 %density.1 = f32[16,256]{1,0:T(8,128)} custom-call(s32[16,512]{1,0:T(8,128)} %broadcast_add_fusion.list_ref, s32[16]{0:T(128)} %and_select_fusion.1.chunks_ref, s32[16]{0:T(128)} %bitcast.1300, s32[144,1,256]{2,1,0:T(1,128)} %copy_select_fusion.pos_ref, bf16[144,2,32,256]{3,2,1,0:T(8,128)(2,1)} %copy-done, bf16[16,32,256]{2,1,0:T(8,128)(2,1)} %stack.1276.target_ref), custom_call_target="tpu_custom_call" | custom-call | tf_op jit(solution)/shard_map/density/pallas_call | solution.py:227
  93.6 1.3 %copy.2748 = f32[1,16,1,256]{3,2,1,0:T(1,128)} copy(f32[1,16,1,256]{3,1,2,0:T(8,128)} %bitcast.1294) | data formatting | bytes 32768 | tf_op jit(solution)/shard_map/reshape | solution.py:242
  (281 shorter events, 6.9 us)
Async XLA Ops:
  1.6 14.2 %collective-permute-start.1 = (f32[4,1,16,1,256]{4,2,3,1,0:T(8,128)S(1)}, f32[4,1,16,1,256]{4,2,3,1,0:T(8,128)S(1)}, u32[]{:S(2)}, u32[]{:S(2)}) collective-permute-start(f32[4,1,16,1,256]{4,2,3,1,0:T(8,128)S(1)} %pad_maximum_fusion.73), channel_id=1, source_target_pairs={{2,0},{4,2},{6,4},{8,6},{10,8},{12,10},{14,12},{16,14},{18,16},{20... | collective-permute-start | bytes 196616 | tf_op jit(solution)/shard_map/ppermute | solution.py:22
  8.6 7.9 %collective-permute-start = (f32[4,1,16,1,256]{4,2,3,1,0:T(8,128)S(1)}, f32[4,1,16,1,256]{4,2,3,1,0:T(8,128)S(1)}, u32[]{:S(2)}, u32[]{:S(2)}) collective-permute-start(f32[4,1,16,1,256]{4,2,3,1,0:T(8,128)S(1)} %pad_maximum_fusion.73), channel_id=1, source_target_pairs={{0,2},{2,4},{4,6},{6,8},{8,10},{10,12},{12,14},{14,16},{16,18},{18... | collective-permute-start | bytes 196616 | tf_op jit(solution)/shard_map/ppermute | solution.py:19
  16.5 1.8 %collective-permute-start.2 = (f32[4,3,16,1,256]{4,2,3,1,0:T(8,128)S(1)}, f32[4,3,16,1,256]{4,2,3,1,0:T(8,128)S(1)}, u32[]{:S(2)}, u32[]{:S(2)}) collective-permute-start(f32[4,3,16,1,256]{4,2,3,1,0:T(8,128)S(1)} %pad_maximum_fusion.72), channel_id=1, source_target_pairs={{0,1},{1,0},{2,3},{3,2},{4,5},{5,4},{6,7},{7,6},{8,9},{9,8},{10,11... | collective-permute-start | bytes 589832 | tf_op jit(solution)/shard_map/ppermute | solution.py:19
  16.6 1.7 %collective-permute-start.3 = (f32[4,3,16,1,256]{4,2,3,1,0:T(8,128)S(1)}, f32[4,3,16,1,256]{4,2,3,1,0:T(8,128)S(1)}, u32[]{:S(2)}, u32[]{:S(2)}) collective-permute-start(f32[4,3,16,1,256]{4,2,3,1,0:T(8,128)S(1)} %pad_maximum_fusion.72), channel_id=1, source_target_pairs={{1,0},{0,1},{3,2},{2,3},{5,4},{4,5},{7,6},{6,7},{9,8},{8,9},{11,10... | collective-permute-start | bytes 589832 | tf_op jit(solution)/shard_map/ppermute | solution.py:22
  48.9 2.2 %copy-start = (bf16[144,2,32,256]{3,2,1,0:T(8,128)(2,1)}, bf16[144,2,32,256]{3,2,1,0:T(8,128)(2,1)S(1)}, u32[]{:S(2)}) copy-start(bf16[144,2,32,256]{3,2,1,0:T(8,128)(2,1)S(1)} %fusion.45.feat_ref) | copy-start | bytes 14155780

commit v2 on v1

v2 whole, which is shorter than its diff:
```python
import functools
import jax
import jax.numpy as jnp
from jax import lax
from jax.experimental import pallas as pl
from jax.experimental.pallas import tpu as pltpu
from jax.sharding import PartitionSpec as P

BLOCK = 16
PER_CHUNK = 8


def extended_2(block, sides, width):
    for axis, dim in sides:
        count = lax.axis_size(axis)
        forward = [(i, (i + 1) % count) for i in range(count)]
        backward = [(target, source) for source, target in forward]
        low = lax.ppermute(
            lax.slice_in_dim(block, block.shape[dim] - width, None, axis=dim), axis, forward
        )
        high = lax.ppermute(lax.slice_in_dim(block, 0, width, axis=dim), axis, backward)
        block = jnp.concatenate([low, block, high], axis=dim)
    return block


def parts(values):
    high = values.astype(jnp.bfloat16).astype(jnp.float32)
    rest = values - high
    middle = rest.astype(jnp.bfloat16).astype(jnp.float32)
    return high, middle, rest - middle


def source_rows(rows):
    high, middle, low = parts(rows)
    zero = jnp.zeros_like(rows)
    return [high, high, high, middle, middle, low, zero, zero]


def target_rows(rows):
    high, middle, low = parts(rows)
    zero = jnp.zeros_like(rows)
    return [high, middle, low, high, middle, high, zero, zero]


def density_kernel(
    rooms, list_ref, chunks_ref, counts_ref, pos_ref, data_ref, out_ref,
    store_ref, mask_ref, sq_a, sq_b,
):
    cells, slots = out_ref.shape
    pairs = pos_ref.shape[0]
    unroll = 4
    zero_block = pairs * rooms
    store_ref[zero_block] = jnp.zeros((BLOCK, 128), jnp.bfloat16)
    lane = lax.broadcasted_iota(jnp.int32, (BLOCK, 128), 1)
    mask_ref[0] = jnp.where(lane < 64, 1.0, 0.0).astype(jnp.bfloat16)
    mask_ref[1] = jnp.where(lane < 64, 0.0, 1.0).astype(jnp.bfloat16)
    row_id = lax.broadcasted_iota(jnp.int32, (rooms * BLOCK, slots), 0)
    row = lax.broadcasted_iota(jnp.int32, (8, slots), 0)

    def assembled(scaled, raw):
        squares = jnp.where(row < 3, scaled * scaled, 0.0)
        norm = jnp.sum(squares, axis=0, keepdims=True)
        rows = jnp.where(row < 3, scaled, raw)
        rows = jnp.where(row == 4, norm, rows)
        return jnp.where(row == 5, 1.0, jnp.where(row > 5, 0.0, rows))

    def compact(step, carry):
        for k in range(unroll):
            pair = step * unroll + k
            relation = pair // cells
            step_y = (relation // 3 - 1).astype(jnp.float32)
            step_z = (relation % 3 - 1).astype(jnp.float32)
            raw = data_ref[pair]
            raw = jnp.concatenate([raw, raw], axis=0)
            offset = jnp.where(row == 0, step_y, jnp.where(row == 2, step_z, 0.0)) - 0.5
            scaled = 4.0 * (raw + offset)
            moved = scaled + jnp.where(row == 1, jnp.where(raw <= 0.5, 4.0, -4.0), 0.0)
            features = jnp.concatenate(
                source_rows(assembled(scaled, raw)) + source_rows(assembled(moved, raw)), axis=0
            ).astype(jnp.bfloat16)
            chosen = jnp.where(row_id == pos_ref[pair], 1.0, 0.0).astype(jnp.bfloat16)
            rows = lax.dot_general(
                chosen, features, (((1,), (1,)), ((), ())), preferred_element_type=jnp.float32
            )
            store_ref[pl.ds(pair * rooms, rooms)] = rows.astype(jnp.bfloat16).reshape(
                rooms, BLOCK, 128
            )
        return carry

    lax.fori_loop(0, pairs // unroll, compact, 0)
    own = (pairs // cells) // 2 * cells
    spread = jnp.where(lax.broadcasted_iota(jnp.int32, (8, 128), 0) == 3, 1.0, 0.0)

    def cell_body(cell, carry):
        raw = data_ref[own + cell]
        raw = jnp.concatenate([raw, raw], axis=0)
        scaled = 4.0 * (raw - 0.5)
        norm = jnp.sum(jnp.where(row < 3, scaled * scaled, 0.0), axis=0, keepdims=True)
        rows = jnp.where(row < 3, -2.0 * scaled, 0.0)
        rows = jnp.where(row == 4, 1.0, jnp.where(row == 5, norm, rows))
        half = target_rows(jnp.concatenate([rows, spread], axis=1))
        weights = jnp.concatenate(half + half, axis=0).astype(jnp.bfloat16)

        def produce(chunk, sq_ref):
            blocks = []
            for k in range(PER_CHUNK):
                entry = list_ref[cell, chunk * PER_CHUNK + k]
                blocks.append(store_ref[entry >> 1] * mask_ref[entry & 1])
            lhs = jnp.concatenate(blocks, axis=0)
            sq_ref[...] = jnp.dot(lhs, weights, preferred_element_type=jnp.float32)

        def consume(sq_ref, acc):
            for group in range(PER_CHUNK * BLOCK // 8):
                rows = pl.ds(group * 8, 8)
                mass = sq_ref[rows, slots:]
                sums = []
                for tile in range(slots // 128):
                    lanes = slice(tile * 128, tile * 128 + 128)
                    squared = jnp.maximum(sq_ref[rows, lanes], 1e-30)
                    q = squared * lax.rsqrt(squared)
                    outer = jnp.maximum(2.0 - q, 0.0)
                    inner = jnp.maximum(outer - 1.0, 0.0)
                    value = outer * outer * outer - 4.0 * (inner * inner * inner)
                    sums.append(acc[tile] + mass * value)
                acc = tuple(sums)
            return acc

        produce(0, sq_a)

        def pair_body(step, acc):
            produce(2 * step + 1, sq_b)
            acc = consume(sq_a, acc)
            produce(2 * step + 2, sq_a)
            return consume(sq_b, acc)

        empty = tuple(jnp.zeros((8, 128), jnp.float32) for _ in range(slots // 128))
        acc = lax.fori_loop(0, (chunks_ref[cell] + 1) // 2, pair_body, empty)
        total = jnp.sum(jnp.concatenate(acc, axis=1), axis=0, keepdims=True)
        total = total * (16.0 / 3.141592653589793)
        slot = lax.broadcasted_iota(jnp.int32, (1, slots), 1)
        out_ref[pl.ds(cell, 1), :] = jnp.where(slot < counts_ref[cell], total, 0.0)
        return carry

    lax.fori_loop(0, cells, cell_body, 0)


def shards(positions, masses, counts, shear_offset):
    cells_y, cells, cells_z, slots = masses.shape
    assert cells_y == 1 and cells_z == 1
    rooms = slots // BLOCK + 1
    slot_index = lax.broadcasted_iota(jnp.int32, masses.shape, 3)
    weight = jnp.where(slot_index < counts[..., None], masses, jnp.float32(0.0))
    data = jnp.stack(
        [positions[0, 0, :, 0], positions[1, 0, :, 0], positions[2, 0, :, 0], weight[0, :, 0]], 1
    )[None, None]
    offset = shear_offset[0]
    shear_index = lax.axis_index("shear")
    cycle = lax.axis_size("shear")
    padded = extended_2(data, (("shear", 0), ("cross", 1)), 1)
    low_shift = jnp.where(shear_index == 0, -offset, 0)
    high_shift = jnp.where(shear_index == cycle - 1, offset, 0)

    masks, shifts = [], []
    for step_y in (-1, 0, 1):
        for step_z in (-1, 0, 1):
            y, x, z, mass = (padded[1 + step_y, 1 + step_z, :, k] for k in range(4))
            keep = mass > 0.0
            for value, step in ((y, step_y), (z, step_z)):
                if step == -1:
                    keep = keep & (value >= 0.5)
                elif step == 1:
                    keep = keep & (value <= 0.5)
            lower = x <= 0.5
            masks.append(jnp.stack([keep & lower, keep & ~lower], 0))
            shifts.append({-1: low_shift, 0: jnp.int32(0), 1: high_shift}[step_y])
    chosen = jnp.stack(masks, 0)
    triangle = (
        lax.broadcasted_iota(jnp.int32, (slots, slots), 0)
        <= lax.broadcasted_iota(jnp.int32, (slots, slots), 1)
    ).astype(jnp.bfloat16)
    ranks = jnp.dot(
        chosen.reshape(-1, slots).astype(jnp.bfloat16), triangle,
        preferred_element_type=jnp.float32,
    ).astype(jnp.int32).reshape(chosen.shape)
    sizes = ranks[..., -1]
    blocks = (sizes + (BLOCK - 1)) // BLOCK
    pos = jnp.where(
        chosen[:, 0],
        ranks[:, 0] - 1,
        jnp.where(chosen[:, 1], ranks[:, 1] - 1 + BLOCK * blocks[:, 0, :, None], -1),
    ).reshape(-1, 1, slots)

    relations = len(masks)
    shift = jnp.stack(shifts)
    target = lax.broadcasted_iota(jnp.int32, (cells, relations, 3), 0)
    relation = lax.broadcasted_iota(jnp.int32, (cells, relations, 3), 1)
    step_x = lax.broadcasted_iota(jnp.int32, (cells, relations, 3), 2) - 1
    cell = (target + step_x + shift[None, :, None] + 2 * cells) % cells
    match = cell[..., None] == jnp.arange(cells, dtype=jnp.int32)
    first = jnp.sum(jnp.where(match, blocks[None, :, 0, None, :], 0), -1)
    second = jnp.sum(jnp.where(match, blocks[None, :, 1, None, :], 0), -1)
    length = jnp.where(step_x == 0, first + second, jnp.where(step_x < 0, second, first))
    variant = jnp.where(step_x == 0, 0, 1)
    start = (relation * cells + cell) * rooms + jnp.where(step_x < 0, first, 0)
    start = 2 * start + variant
    length = length.reshape(cells, -1)
    start = start.reshape(cells, -1)
    end = jnp.cumsum(length, axis=1)
    begin = end - length
    room = relations * 3 * rooms + 3 * PER_CHUNK
    room = (room + 127) // 128 * 128
    index = lax.broadcasted_iota(jnp.int32, (cells, relations * 3, room), 2)
    inside = (index >= begin[..., None]) & (index < end[..., None])
    zero_block = 2 * relations * cells * rooms
    block_list = zero_block + jnp.sum(
        jnp.where(inside, (start - 2 * begin)[..., None] + 2 * index - zero_block, 0), 1
    )
    chunks = (end[:, -1] + (PER_CHUNK - 1)) // PER_CHUNK

    smem = pl.BlockSpec(memory_space=pltpu.SMEM)
    vmem = pl.BlockSpec(memory_space=pltpu.VMEM)
    rows = PER_CHUNK * BLOCK
    density = pl.pallas_call(
        functools.partial(density_kernel, rooms),
        out_shape=jax.ShapeDtypeStruct((cells, slots), jnp.float32),
        in_specs=[smem, smem, smem, vmem, vmem],
        out_specs=vmem,
        scratch_shapes=[
            pltpu.VMEM((relations * cells * rooms + 1, BLOCK, 128), jnp.bfloat16),
            pltpu.VMEM((2, BLOCK, 128), jnp.bfloat16),
            pltpu.VMEM((rows, slots + 128), jnp.float32),
            pltpu.VMEM((rows, slots + 128), jnp.float32),
        ],
        compiler_params=pltpu.CompilerParams(vmem_limit_bytes=56 * 1024 * 1024),
        name="density",
    )(block_list, chunks, counts.reshape(-1), pos, padded.reshape(-1, 4, slots))
    return density.reshape(masses.shape)


def solution(mesh):
    in_specs = (
        P(None, "shear", None, "cross", None),
        P("shear", None, "cross", None),
        P("shear", None, "cross"),
        P(),
    )
    out_specs = P("shear", None, "cross", None)
    return jax.shard_map(shards, mesh=mesh, in_specs=in_specs, out_specs=out_specs, check_vma=False)
```

time: 95.8 us -> 65.6 us (0.68); the launches traced: 94.9 us -> 66.1 us
  other arithmetic: 29.5 us -> 4.71 us
  waiting for transfers between devices: 0.8 us -> 7.31 us
  local copies, waits for them, and re-layouts: 11.6 us -> 5.75 us
  Pallas kernels: 42.5 us -> 39.6 us
  between operations: 2.65 us -> 0.96 us
    unnamed x16 -> x8, other arithmetic: 19.2 us -> 0.07 us
    another operation x177 -> x2, local copies, waits for them, and re-layouts: 5.61 us -> 0.01 us  [the longest x1 0.01 us: shards(): jnp.stack([positions[0, 0, :, 0], positions[1, 0, :, 0], positions[2, 0,...]
    ppermute x2, waiting for transfers between devices: 0.7 us -> 6.16 us  [extended_2(): lax.ppermute(lax.slice_in_dim(block, block.shape[dim] - width, None, axis...]
    pallas_call x1, Pallas kernels: 42.5 us -> 39.6 us  [shards(): pl.pallas_call(functools.partial(density_kernel, rooms), out_shape=jax.Sh...]
    concatenate x2 -> x0, other arithmetic: 2.36 us -> none  [the longest x1 2.36 us: shards(): features = jnp.concatenate(features, 0)]
    unnamed x8 -> x10, local copies, waits for them, and re-layouts: 3.42 us -> 1.18 us
    another operation x31 -> x1, other arithmetic: 1.84 us -> 0.07 us  [shards(): jnp.stack([positions[0, 0, :, 0], positions[1, 0, :, 0], positions[2, 0,...]
    concatenate x0 -> x1, local copies, waits for them, and re-layouts: none -> 1.2 us  [extended_2(): block = jnp.concatenate([low, block, high], axis=dim)]
  transfers between devices with their start and end apart: 4 -> 4, of which waited for: 2 -> 4; matrix products, arithmetic and copies ran while one was open for 7% -> 2% of each run, Pallas kernels for 0% -> 0%
where the time goes in v2:
time: 65.6 us; the launch traced here: 66.1 us
  Pallas kernels  39.6 us (60%)
  starting transfers between devices  7.58 us (12%)
  waiting for transfers between devices  7.31 us (11%)
  local copies, waits for them, and re-layouts  5.75 us (9%)
  other arithmetic  4.71 us (7%)
  between operations  0.96 us (1%)
    pallas_call x1, Pallas kernels, shards(): pl.pallas_call(functools.partial(density_kernel, rooms), out_shape=jax.Sh...  39.6 us
    ppermute x2, starting transfers between devices, extended_2(): lax.ppermute(lax.slice_in_dim(block, 0, width, axis=dim), axis, backward)  7.08 us
    ppermute x2, waiting for transfers between devices, extended_2(): lax.ppermute(lax.slice_in_dim(block, block.shape[dim] - width, None, axis...  6.16 us
    reshape x1, local copies, waits for them, and re-layouts, shards(): return density.reshape(masses.shape)  1.34 us
  transfers between devices with their start and end apart: 4, of which 4 were waited for; matrix products, arithmetic and copies ran while one was open for 2% of the time, Pallas kernels for 0%

profile of v2, /device:TPU:0, one launch (start us, length us, event | category | flops | bytes accessed | tf_op | source)
XLA Modules:
  0.0 66.1 jit_solution(1407500689106779813)
XLA Ops:
  0.0 0.8 %fusion.78 = (f32[1,1,16,1,256]{4,3,2,1,0:T(1,128)S(1)}, f32[1,1,16,1,256]{4,3,2,1,0:T(1,128)S(1)}, f32[1,1,16,1,256]{4,3,2,1,0:T(1,128)S(1)}) fusion(f32[3,1,16,1,256]{4,3,2,1,0:T(1,128)} %param.4), kind=kLoop, calls=%fused_computation.157 | loop fusion | bytes 98304 | tf_op jit(solution)/shard_map/slice | solution.py:154
  0.8 0.7 %copy-done = f32[1,16,1,256]{3,2,1,0:T(1,128)S(1)} copy-done((f32[1,16,1,256]{3,2,1,0:T(1,128)S(1)}, f32[1,16,1,256]{3,2,1,0:T(1,128)}, u32[]{:S(2)}) %copy-start) | copy-done | bytes 16408
  1.6 7.0 %collective-permute-start.1 = (f32[1,1,16,4,256]{4,2,3,1,0:T(8,128)S(1)}, f32[1,1,16,4,256]{4,2,3,1,0:T(8,128)S(1)}, u32[]{:S(2)}, u32[]{:S(2)}) collective-permute-start(f32[1,1,16,4,256]{4,2,3,1,0:T(8,128)S(1)} %maximum_bitcast_fusion), channel_id=1, source_target_pairs={{2,0},{4,2},{6,4},{8,6},{10,8},{12,10},{14,12},{16,14},{18,16},{20... | collective-permute-start | bytes 196616 | tf_op jit(solution)/shard_map/ppermute | solution.py:21
  10.0 0.1 add_select_fusion
  10.2 0.3 collective-permute-done.1
  10.5 6.0 %collective-permute-done = f32[1,1,16,4,256]{4,2,3,1,0:T(8,128)S(1)} collective-permute-done((f32[1,1,16,4,256]{4,2,3,1,0:T(8,128)S(1)}, f32[1,1,16,4,256]{4,2,3,1,0:T(8,128)S(1)}, u32[]{:S(2)}, u32[]{:S(2)}) %collective-permute-start) | collective-permute-done | bytes 65568 | tf_op jit(solution)/shard_map/ppermute | solution.py:18
  16.5 0.5 collective-permute-start.2
  17.1 0.9 %collective-permute-done.3 = f32[3,1,16,4,256]{4,2,3,1,0:T(8,128)S(1)} collective-permute-done((f32[3,1,16,4,256]{4,2,3,1,0:T(8,128)S(1)}, f32[3,1,16,4,256]{4,2,3,1,0:T(8,128)S(1)}, u32[]{:S(2)}, u32[]{:S(2)}) %collective-permute-start.3) | collective-permute-done | bytes 196640 | tf_op jit(solution)/shard_map/ppermute | solution.py:21
  18.0 0.2 collective-permute-done.2
  18.5 0.2 convolution_convert_fusion
  18.7 0.1 slice_add_fusion.2
  18.8 0.2 copy.57
  19.1 1.1 %select_reduce_fusion.2 = (s32[16,9,3]{0,2,1:T(4,128)S(1)}, s32[16,9,3]{0,2,1:T(4,128)S(1)}) fusion(s32[9,16]{1,0:T(8,128)S(1)} %bitcast.147, s32[16,9,3]{0,2,1:T(4,128)S(1)} %add_select_fusion, s32[9,16]{1,0:T(8,128)S(1)} %bitcast.146), kind=kLoop, calls=%fused_computation.10 | loop fusion | flops 33696 | bytes 6336 | tf_op jit(solution)/shard_map/reduce_sum | solution.py:200
  20.4 0.2 reduce_window_sum.11
  20.6 0.2 fusion.49
  20.9 1.2 %copy.47 = f32[3,3,16,4,256]{4,3,2,1,0:T(4,128)} copy(f32[3,3,16,4,256]{4,2,3,1,0:T(8,128)S(1)} %pad_maximum_fusion) | data formatting | bytes 1179648 | tf_op jit(solution)/shard_map/concatenate | solution.py:22
  22.1 0.2 copy.58
  22.3 0.5 and_select_fusion.1.chunks_ref
  23.1 0.3 select_reduce_fusion
  23.3 0.6 broadcast_add_fusion.list_ref
  23.9 0.2 copy.59
  24.1 1.1 %copy_select_fusion.pos_ref = s32[144,1,256]{2,1,0:T(1,128)} fusion(pred[144,1,256]{2,0,1:T(8,128)(4,1)S(1)} %bitcast.143, pred[144,1,256]{2,0,1:T(8,128)(4,1)S(1)} %bitcast.142, s32[9,1,16,256]{3,1,2,0:T(1,128)S(1)} %copy.59, s32[9,1,16,256]{3,1,2,0:T(1,128)S(1)} %copy.58, s32[144]{0:T(256)S(1)} %mul.69), kind=kLoop, calls=%fused_computation.6 | loop fusion | flops 110592 | bytes 516672 | tf_op jit(solution)/shard_map/jit(_where)/select_n | solution.py:187
  25.2 39.6 %density.1 = f32[16,256]{1,0:T(8,128)} custom-call(s32[16,512]{1,0:T(8,128)} %broadcast_add_fusion.list_ref, s32[16]{0:T(128)} %and_select_fusion.1.chunks_ref, s32[16]{0:T(128)} %bitcast.148, s32[144,1,256]{2,1,0:T(1,128)} %copy_select_fusion.pos_ref, f32[144,4,256]{2,1,0:T(4,128)} %bitcast.138), custom_call_target="tpu_custom_call" | custom-call | tf_op jit(solution)/shard_map/density/pallas_call | solution.py:223
  64.8 1.3 %copy.48 = f32[1,16,1,256]{3,2,1,0:T(1,128)} copy(f32[1,16,1,256]{3,1,2,0:T(8,128)} %bitcast.144) | data formatting | bytes 32768 | tf_op jit(solution)/shard_map/reshape | solution.py:237
  (70 shorter events, 1.9 us)
Async XLA Ops:
  0.8 0.7 %copy-start = (f32[1,16,1,256]{3,2,1,0:T(1,128)S(1)}, f32[1,16,1,256]{3,2,1,0:T(1,128)}, u32[]{:S(2)}) copy-start(f32[1,16,1,256]{3,2,1,0:T(1,128)} %param.5) | copy-start | bytes 49156
  0.8 0.7 %copy-start.1 = (s32[1,16,1]{1,2,0:T(1,128)S(1)}, s32[1,16,1]{1,2,0:T(1,128)}, u32[]{:S(2)}) copy-start(s32[1,16,1]{1,2,0:T(1,128)} %param.6) | copy-start | bytes 196
  1.6 8.9 %collective-permute-start.1 = (f32[1,1,16,4,256]{4,2,3,1,0:T(8,128)S(1)}, f32[1,1,16,4,256]{4,2,3,1,0:T(8,128)S(1)}, u32[]{:S(2)}, u32[]{:S(2)}) collective-permute-start(f32[1,1,16,4,256]{4,2,3,1,0:T(8,128)S(1)} %maximum_bitcast_fusion), channel_id=1, source_target_pairs={{2,0},{4,2},{6,4},{8,6},{10,8},{12,10},{14,12},{16,14},{18,16},{20... | collective-permute-start | bytes 196616 | tf_op jit(solution)/shard_map/ppermute | solution.py:21
  8.6 7.9 %collective-permute-start = (f32[1,1,16,4,256]{4,2,3,1,0:T(8,128)S(1)}, f32[1,1,16,4,256]{4,2,3,1,0:T(8,128)S(1)}, u32[]{:S(2)}, u32[]{:S(2)}) collective-permute-start(f32[1,1,16,4,256]{4,2,3,1,0:T(8,128)S(1)} %maximum_bitcast_fusion), channel_id=1, source_target_pairs={{0,2},{2,4},{4,6},{6,8},{8,10},{10,12},{12,14},{14,16},{16,18},{18... | collective-permute-start | bytes 196616 | tf_op jit(solution)/shard_map/ppermute | solution.py:18
  16.5 1.5 %collective-permute-start.3 = (f32[3,1,16,4,256]{4,2,3,1,0:T(8,128)S(1)}, f32[3,1,16,4,256]{4,2,3,1,0:T(8,128)S(1)}, u32[]{:S(2)}, u32[]{:S(2)}) collective-permute-start(f32[3,1,16,4,256]{4,2,3,1,0:T(8,128)S(1)} %pad_maximum_fusion.1), channel_id=1, source_target_pairs={{1,0},{0,1},{3,2},{2,3},{5,4},{4,5},{7,6},{6,7},{9,8},{8,9},{11,10... | collective-permute-start | bytes 589832 | tf_op jit(solution)/shard_map/ppermute | solution.py:21
  16.5 1.7 %collective-permute-start.2 = (f32[3,1,16,4,256]{4,2,3,1,0:T(8,128)S(1)}, f32[3,1,16,4,256]{4,2,3,1,0:T(8,128)S(1)}, u32[]{:S(2)}, u32[]{:S(2)}) collective-permute-start(f32[3,1,16,4,256]{4,2,3,1,0:T(8,128)S(1)} %pad_maximum_fusion.1), channel_id=1, source_target_pairs={{0,1},{1,0},{2,3},{3,2},{4,5},{5,4},{6,7},{7,6},{8,9},{9,8},{10,11... | collective-permute-start | bytes 589832 | tf_op jit(solution)/shard_map/ppermute | solution.py:18

commit v3 on v2

--- a/solution.py
+++ b/solution.py
@@ -10,17 +10,60 @@
 PER_CHUNK = 8
 
 
-def extended_2(block, sides, width):
-    for axis, dim in sides:
-        count = lax.axis_size(axis)
-        forward = [(i, (i + 1) % count) for i in range(count)]
-        backward = [(target, source) for source, target in forward]
-        low = lax.ppermute(
-            lax.slice_in_dim(block, block.shape[dim] - width, None, axis=dim), axis, forward
+def halo_kernel(data_ref, out_ref, send_sems, recv_sems, local_sem):
+    shear, cross = lax.axis_index("shear"), lax.axis_index("cross")
+    rows, planes = lax.axis_size("shear"), lax.axis_size("cross")
+    mesh_ids = pl.DeviceIdType.MESH
+    along_y = [(lax.rem(shear + rows - step, rows), cross) for step in (-1, 1)]
+    along_z = [(shear, lax.rem(cross + planes - step, planes)) for step in (-1, 1)]
+    barrier = pltpu.get_barrier_semaphore()
+    for device in along_y + along_z:
+        pl.semaphore_signal(barrier, inc=1, device_id=device, device_id_type=mesh_ids)
+    own = pltpu.make_async_copy(data_ref, out_ref.at[1, 1], local_sem)
+    own.start()
+    pl.semaphore_wait(barrier, 4)
+
+    def sent(source, y, z, device):
+        slot = 3 * y + z
+        copy = pltpu.make_async_remote_copy(
+            src_ref=source,
+            dst_ref=out_ref.at[y, z],
+            send_sem=send_sems.at[slot],
+            recv_sem=recv_sems.at[slot],
+            device_id=device,
+            device_id_type=mesh_ids,
         )
-        high = lax.ppermute(lax.slice_in_dim(block, 0, width, axis=dim), axis, backward)
-        block = jnp.concatenate([low, block, high], axis=dim)
-    return block
+        copy.start()
+        return copy
+
+    rows_sent = [sent(data_ref, y, 1, along_y[k]) for k, y in enumerate((0, 2))]
+    planes_sent = [sent(data_ref, 1, z, along_z[k]) for k, z in enumerate((0, 2))]
+    for k, y in enumerate((0, 2)):
+        rows_sent[k].wait_recv()
+        for j, z in enumerate((0, 2)):
+            planes_sent.append(sent(out_ref.at[y, 1], y, z, along_z[j]))
+    for copy in rows_sent:
+        copy.wait_send()
+    for copy in planes_sent:
+        copy.wait()
+    own.wait()
+
+
+def halo(data):
+    vmem = pl.BlockSpec(memory_space=pltpu.VMEM)
+    return pl.pallas_call(
+        halo_kernel,
+        out_shape=jax.ShapeDtypeStruct((3, 3) + data.shape, data.dtype),
+        in_specs=[vmem],
+        out_specs=vmem,
+        scratch_shapes=[
+            pltpu.SemaphoreType.DMA((9,)),
+            pltpu.SemaphoreType.DMA((9,)),
+            pltpu.SemaphoreType.DMA,
+        ],
+        compiler_params=pltpu.CompilerParams(collective_id=0, has_side_effects=True),
+        name="halo",
+    )(data)
 
 
 def parts(values):
@@ -43,7 +86,7 @@
 
 
 def density_kernel(
-    rooms, list_ref, chunks_ref, counts_ref, pos_ref, data_ref, out_ref,
+    rooms, list_ref, chunks_ref, counts_ref, used_ref, pos_ref, data_ref, out_ref,
     store_ref, mask_ref, sq_a, sq_b,
 ):
     cells, slots = out_ref.shape
@@ -64,7 +107,22 @@
         rows = jnp.where(row == 4, norm, rows)
         return jnp.where(row == 5, 1.0, jnp.where(row > 5, 0.0, rows))
 
+    first_rooms = rooms // 2 + 2
+
+    def fill(batch, begin, count):
+        for pair, features in batch:
+            chosen = jnp.where(
+                row_id[: count * BLOCK] == pos_ref[pair] - begin * BLOCK, 1.0, 0.0
+            ).astype(jnp.bfloat16)
+            rows = lax.dot_general(
+                chosen, features, (((1,), (1,)), ((), ())), preferred_element_type=jnp.float32
+            )
+            store_ref[pl.ds(pair * rooms + begin, count)] = rows.astype(jnp.bfloat16).reshape(
+                count, BLOCK, 128
+            )
+
     def compact(step, carry):
+        batch = []
         for k in range(unroll):
             pair = step * unroll + k
             relation = pair // cells
@@ -78,13 +136,16 @@
             features = jnp.concatenate(
                 source_rows(assembled(scaled, raw)) + source_rows(assembled(moved, raw)), axis=0
             ).astype(jnp.bfloat16)
-            chosen = jnp.where(row_id == pos_ref[pair], 1.0, 0.0).astype(jnp.bfloat16)
-            rows = lax.dot_general(
-                chosen, features, (((1,), (1,)), ((), ())), preferred_element_type=jnp.float32
-            )
-            store_ref[pl.ds(pair * rooms, rooms)] = rows.astype(jnp.bfloat16).reshape(
-                rooms, BLOCK, 128
-            )
+            batch.append((pair, features))
+        fill(batch, 0, first_rooms)
+        most = used_ref[step * unroll]
+        for k in range(1, unroll):
+            most = jnp.maximum(most, used_ref[step * unroll + k])
+
+        @pl.when(most > first_rooms)
+        def _():
+            fill(batch, first_rooms, rooms - first_rooms)
+
         return carry
 
     lax.fori_loop(0, pairs // unroll, compact, 0)
@@ -152,11 +213,11 @@
     weight = jnp.where(slot_index < counts[..., None], masses, jnp.float32(0.0))
     data = jnp.stack(
         [positions[0, 0, :, 0], positions[1, 0, :, 0], positions[2, 0, :, 0], weight[0, :, 0]], 1
-    )[None, None]
+    )
     offset = shear_offset[0]
     shear_index = lax.axis_index("shear")
     cycle = lax.axis_size("shear")
-    padded = extended_2(data, (("shear", 0), ("cross", 1)), 1)
+    padded = halo(data)
     low_shift = jnp.where(shear_index == 0, -offset, 0)
     high_shift = jnp.where(shear_index == cycle - 1, offset, 0)
 
@@ -223,7 +284,7 @@
     density = pl.pallas_call(
         functools.partial(density_kernel, rooms),
         out_shape=jax.ShapeDtypeStruct((cells, slots), jnp.float32),
-        in_specs=[smem, smem, smem, vmem, vmem],
+        in_specs=[smem, smem, smem, smem, vmem, vmem],
         out_specs=vmem,
         scratch_shapes=[
             pltpu.VMEM((relations * cells * rooms + 1, BLOCK, 128), jnp.bfloat16),
@@ -233,7 +294,7 @@
         ],
         compiler_params=pltpu.CompilerParams(vmem_limit_bytes=56 * 1024 * 1024),
         name="density",
-    )(block_list, chunks, counts.reshape(-1), pos, padded.reshape(-1, 4, slots))
+    )(block_list, chunks, counts.reshape(-1), jnp.sum(blocks, 1).reshape(-1), pos, padded.reshape(-1, 4, slots))
     return density.reshape(masses.shape)
 
 

time: 65.6 us -> 65.5 us (level); the launches traced: 66.1 us -> 65 us
  Pallas kernels: 39.6 us -> 50.9 us
  starting transfers between devices: 7.58 us -> 0 us
  waiting for transfers between devices: 7.31 us -> 0 us
  other arithmetic: 4.71 us -> 8.81 us
  local copies, waits for them, and re-layouts: 5.75 us -> 4.11 us
    pallas_call x0 -> x1, Pallas kernels: none -> 12.7 us  [halo(): pl.pallas_call(halo_kernel, out_shape=jax.ShapeDtypeStruct((3, 3) + data....]
    ppermute x4 -> x0, starting transfers between devices: 7.58 us -> none  [the longest x2 7.08 us: extended_2(): lax.ppermute(lax.slice_in_dim(block, 0, width, axis=dim), axis, backward)]
    ppermute x4 -> x0, waiting for transfers between devices: 7.31 us -> none  [the longest x2 6.16 us: extended_2(): lax.ppermute(lax.slice_in_dim(block, block.shape[dim] - width, None, axis...]
    le x0 -> x2, other arithmetic: none -> 3.41 us  [shards(): lower = x <= 0.5]
    pallas_call x1, Pallas kernels: 39.6 us -> 38.2 us  [shards(): pl.pallas_call(functools.partial(density_kernel, rooms), out_shape=jax.Sh...]
    concatenate x1 -> x0, local copies, waits for them, and re-layouts: 1.2 us -> none  [extended_2(): block = jnp.concatenate([low, block, high], axis=dim)]
    slice x1 -> x0, local copies, waits for them, and re-layouts: 0.76 us -> none  [shards(): positions[0, 0, :, 0]]
    another operation x1 -> x2, other arithmetic: 0.07 us -> 0.77 us  [shards(): jnp.stack([positions[0, 0, :, 0], positions[1, 0, :, 0], positions[2, 0,...]
  transfers between devices with their start and end apart: 4 -> 0, of which waited for: 4 -> 0; matrix products, arithmetic and copies ran while one was open for 2% -> 0% of each run, Pallas kernels for 0% -> 0%
where the time goes in v3:
time: 65.5 us; the launch traced here: 65 us
  Pallas kernels  50.9 us (78%)
  other arithmetic  8.81 us (13%)
  local copies, waits for them, and re-layouts  4.11 us (6%)
  between operations  0.99 us (2%)
    pallas_call x1, Pallas kernels, shards(): pl.pallas_call(functools.partial(density_kernel, rooms), out_shape=jax.Sh...  38.2 us
    pallas_call x1, Pallas kernels, halo(): pl.pallas_call(halo_kernel, out_shape=jax.ShapeDtypeStruct((3, 3) + data....  12.7 us
    le x2, other arithmetic, shards(): lower = x <= 0.5  3.41 us
    reshape x1, local copies, waits for them, and re-layouts, shards(): return density.reshape(masses.shape)  1.34 us

profile of v3, /device:TPU:0, one launch (start us, length us, event | category | flops | bytes accessed | tf_op | source)
XLA Modules:
  0.0 65.0 jit_solution(7608577353470023695)
XLA Ops:
  0.8 0.1 iota.108
  0.9 0.1 iota.100
  1.5 0.4 copy-done.1
  2.0 0.1 add_select_fusion
  2.1 0.7 %pad_maximum_fusion.data_ref = f32[16,4,256]{2,1,0:T(4,128)} fusion(f32[16,1,256]{2,1,0:T(1,128)S(1)} %fusion.11, f32[16,1,256]{2,1,0:T(1,128)S(1)} %get-tuple-element.61, f32[16,1,256]{2,1,0:T(1,128)S(1)} %get-tuple-element.62, f32[16,1,256]{2,1,0:T(1,128)S(1)} %get-tuple-element.60), kind=kLoop, calls=%fused_computation.15 | loop fusion | flops 49152 | bytes 131072 | tf_op jit(solution)/shard_map/stack | solution.py:214
  2.8 12.7 %halo.1 = f32[3,3,16,4,256]{4,3,2,1,0:T(4,128)} custom-call(f32[16,4,256]{2,1,0:T(4,128)} %pad_maximum_fusion.data_ref), custom_call_target="tpu_custom_call" | custom-call | tf_op jit(solution)/shard_map/halo/pallas_call | solution.py:54
  15.5 1.4 %slice_compare_fusion.2 = (pred[1,1,16,1,256]{4,3,2,1,0:T(4,128)(4,1)S(1)}, pred[1,1,16,1,256]{4,3,2,1,0:T(4,128)(4,1)S(1)}, pred[1,1,16,1,256]{4,3,2,1,0:T(4,12...) fusion(f32[3,3,16,4,256]{4,3,2,1,0:T(4,128)} %halo.1), kind=kLoop, calls=%fused_computation.52 | loop fusion | flops 65536 | bytes 204800 | tf_op jit(solution)/shard_map/le | solution.py:234
  17.1 2.0 %slice_compare_fusion = (pred[1,1,16,1,256]{4,3,2,1,0:T(4,128)(4,1)S(1)}, pred[1,1,16,1,256]{4,3,2,1,0:T(4,128)(4,1)S(1)}, pred[1,1,16,1,256]{4,3,2,1,0:T(4,128)...) fusion(f32[3,3,16,4,256]{4,3,2,1,0:T(4,128)} %halo.1), kind=kLoop, calls=%fused_computation.50 | loop fusion | flops 106496 | bytes 360448 | tf_op jit(solution)/shard_map/le | solution.py:234
  19.3 0.2 convolution_convert_fusion
  19.5 0.1 slice_add_fusion.2
  19.6 0.2 copy.637
  19.8 0.2 copy.638
  20.1 0.6 reshape.949.used_ref
  20.8 1.1 %select_reduce_fusion.2 = (s32[16,9,3]{0,2,1:T(4,128)S(1)}, s32[16,9,3]{0,2,1:T(4,128)S(1)}) fusion(s32[9,16]{1,0:T(8,128)S(1)} %bitcast.162, s32[16,9,3]{0,2,1:T(4,128)S(1)} %add_select_fusion, s32[9,16]{1,0:T(8,128)S(1)} %bitcast.161), kind=kLoop, calls=%fused_computation.9 | loop fusion | flops 33696 | bytes 6336 | tf_op jit(solution)/shard_map/reduce_sum | solution.py:261
  22.1 0.2 reduce_window_sum.11
  22.3 0.2 fusion.28
  22.5 0.6 and_select_fusion.1.chunks_ref
  23.1 0.1 copy.606
  23.4 0.3 select_reduce_fusion
  23.6 0.6 broadcast_add_fusion.list_ref
  24.3 0.2 copy.639
  24.4 1.1 %copy_select_fusion.pos_ref = s32[144,1,256]{2,1,0:T(1,128)} fusion(pred[144,1,256]{2,0,1:T(8,128)(4,1)S(1)} %bitcast.159, pred[144,1,256]{2,0,1:T(8,128)(4,1)S(1)} %bitcast.158, s32[9,1,16,256]{3,1,2,0:T(1,128)S(1)} %copy.639, s32[9,1,16,256]{3,1,2,0:T(1,128)S(1)} %copy.638, s32[144]{0:T(256)S(1)} %mul.69), kind=kLoop, calls=%fused_computation.5 | loop fusion | flops 110592 | bytes 516672 | tf_op jit(solution)/shard_map/jit(_where)/select_n | solution.py:248
  25.5 38.2 %density.1 = f32[16,256]{1,0:T(8,128)} custom-call(s32[16,512]{1,0:T(8,128)} %broadcast_add_fusion.list_ref, s32[16]{0:T(128)} %and_select_fusion.1.chunks_ref, s32[16]{0:T(128)} %bitcast.163, s32[144]{0:T(256)} %reshape.949.used_ref, s32[144,1,256]{2,1,0:T(1,128)} %copy_select_fusion.pos_ref, f32[144,4,256]{2,1,0:T(4,128)} %bitcast.154), custom_call_target="tpu_custom_call" | custom-call | tf_op jit(solution)/shard_map/density/pallas_call | solution.py:284
  63.7 1.3 %copy.613 = f32[1,16,1,256]{3,2,1,0:T(1,128)} copy(f32[1,16,1,256]{3,1,2,0:T(8,128)} %bitcast.160) | data formatting | bytes 32768 | tf_op jit(solution)/shard_map/reshape | solution.py:298
  (63 shorter events, 1.5 us)
Async XLA Ops:
  1.2 0.7 %copy-start.1 = (f32[1,16,1,256]{3,2,1,0:T(1,128)S(1)}, f32[1,16,1,256]{3,2,1,0:T(1,128)}, u32[]{:S(2)}) copy-start(f32[1,16,1,256]{3,2,1,0:T(1,128)} %param.5) | copy-start | bytes 49156
  1.2 0.7 %copy-start.2 = (s32[1,16,1]{1,2,0:T(1,128)S(1)}, s32[1,16,1]{1,2,0:T(1,128)}, u32[]{:S(2)}) copy-start(s32[1,16,1]{1,2,0:T(1,128)} %param.6) | copy-start | bytes 196
  1.2 0.9 %copy-start = (f32[3,1,16,1,256]{4,3,2,1,0:T(1,128)S(1)}, f32[3,1,16,1,256]{4,3,2,1,0:T(1,128)}, u32[]{:S(2)}) copy-start(f32[3,1,16,1,256]{4,3,2,1,0:T(1,128)} %param.4) | copy-start | bytes 147460

commit v4 on v3

--- a/solution.py
+++ b/solution.py
@@ -152,14 +152,14 @@
     own = (pairs // cells) // 2 * cells
     spread = jnp.where(lax.broadcasted_iota(jnp.int32, (8, 128), 0) == 3, 1.0, 0.0)
 
-    def cell_body(cell, carry):
+    def cell_body(cell, width):
         raw = data_ref[own + cell]
         raw = jnp.concatenate([raw, raw], axis=0)
         scaled = 4.0 * (raw - 0.5)
         norm = jnp.sum(jnp.where(row < 3, scaled * scaled, 0.0), axis=0, keepdims=True)
         rows = jnp.where(row < 3, -2.0 * scaled, 0.0)
         rows = jnp.where(row == 4, 1.0, jnp.where(row == 5, norm, rows))
-        half = target_rows(jnp.concatenate([rows, spread], axis=1))
+        half = target_rows(jnp.concatenate([rows[:, :width], spread], axis=1))
         weights = jnp.concatenate(half + half, axis=0).astype(jnp.bfloat16)
 
         def produce(chunk, sq_ref):
@@ -168,14 +168,14 @@
                 entry = list_ref[cell, chunk * PER_CHUNK + k]
                 blocks.append(store_ref[entry >> 1] * mask_ref[entry & 1])
             lhs = jnp.concatenate(blocks, axis=0)
-            sq_ref[...] = jnp.dot(lhs, weights, preferred_element_type=jnp.float32)
+            sq_ref[:, : width + 128] = jnp.dot(lhs, weights, preferred_element_type=jnp.float32)
 
         def consume(sq_ref, acc):
             for group in range(PER_CHUNK * BLOCK // 8):
                 rows = pl.ds(group * 8, 8)
-                mass = sq_ref[rows, slots:]
+                mass = sq_ref[rows, width : width + 128]
                 sums = []
-                for tile in range(slots // 128):
+                for tile in range(width // 128):
                     lanes = slice(tile * 128, tile * 128 + 128)
                     squared = jnp.maximum(sq_ref[rows, lanes], 1e-30)
                     q = squared * lax.rsqrt(squared)
@@ -194,15 +194,27 @@
             produce(2 * step + 2, sq_a)
             return consume(sq_b, acc)
 
-        empty = tuple(jnp.zeros((8, 128), jnp.float32) for _ in range(slots // 128))
+        empty = tuple(jnp.zeros((8, 128), jnp.float32) for _ in range(width // 128))
         acc = lax.fori_loop(0, (chunks_ref[cell] + 1) // 2, pair_body, empty)
         total = jnp.sum(jnp.concatenate(acc, axis=1), axis=0, keepdims=True)
         total = total * (16.0 / 3.141592653589793)
+        if width < slots:
+            total = jnp.concatenate([total, jnp.zeros((1, slots - width), jnp.float32)], axis=1)
         slot = lax.broadcasted_iota(jnp.int32, (1, slots), 1)
         out_ref[pl.ds(cell, 1), :] = jnp.where(slot < counts_ref[cell], total, 0.0)
+
+    def sized_body(cell, carry):
+        @pl.when(counts_ref[cell] <= 128)
+        def _():
+            cell_body(cell, 128)
+
+        @pl.when(counts_ref[cell] > 128)
+        def _():
+            cell_body(cell, slots)
+
         return carry
 
-    lax.fori_loop(0, cells, cell_body, 0)
+    lax.fori_loop(0, cells, sized_body, 0)
 
 
 def shards(positions, masses, counts, shear_offset):
@@ -221,20 +233,16 @@
     low_shift = jnp.where(shear_index == 0, -offset, 0)
     high_shift = jnp.where(shear_index == cycle - 1, offset, 0)
 
-    masks, shifts = [], []
-    for step_y in (-1, 0, 1):
-        for step_z in (-1, 0, 1):
-            y, x, z, mass = (padded[1 + step_y, 1 + step_z, :, k] for k in range(4))
-            keep = mass > 0.0
-            for value, step in ((y, step_y), (z, step_z)):
-                if step == -1:
-                    keep = keep & (value >= 0.5)
-                elif step == 1:
-                    keep = keep & (value <= 0.5)
-            lower = x <= 0.5
-            masks.append(jnp.stack([keep & lower, keep & ~lower], 0))
-            shifts.append({-1: low_shift, 0: jnp.int32(0), 1: high_shift}[step_y])
-    chosen = jnp.stack(masks, 0)
+    relations = 9
+    values = padded.reshape(relations, cells, 4, slots)
+    y, x, z, mass = (values[:, :, k] for k in range(4))
+    which = lax.broadcasted_iota(jnp.int32, y.shape, 0)
+    keep = mass > 0.0
+    for value, step in ((y, which // 3 - 1), (z, which % 3 - 1)):
+        keep = keep & ((step != -1) | (value >= 0.5)) & ((step != 1) | (value <= 0.5))
+    lower = x <= 0.5
+    chosen = jnp.stack([keep & lower, keep & ~lower], 1)
+    shifts = [low_shift] * 3 + [jnp.int32(0)] * 3 + [high_shift] * 3
     triangle = (
         lax.broadcasted_iota(jnp.int32, (slots, slots), 0)
         <= lax.broadcasted_iota(jnp.int32, (slots, slots), 1)
@@ -251,7 +259,6 @@
         jnp.where(chosen[:, 1], ranks[:, 1] - 1 + BLOCK * blocks[:, 0, :, None], -1),
     ).reshape(-1, 1, slots)
 
-    relations = len(masks)
     shift = jnp.stack(shifts)
     target = lax.broadcasted_iota(jnp.int32, (cells, relations, 3), 0)
     relation = lax.broadcasted_iota(jnp.int32, (cells, relations, 3), 1)

time: 65.5 us -> 68.5 us (1.046)
  local copies, waits for them, and re-layouts: 4.11 us -> 8.45 us
  Pallas kernels: 50.9 us -> 49.6 us
    le x2 -> x0, other arithmetic: 3.41 us -> none  [shards(): lower = x <= 0.5]
    select_n x1, other arithmetic: 1.07 us -> 3.61 us  [shards(): jnp.where(chosen[:, 0], ranks[:, 0] - 1, jnp.where(chosen[:, 1], ranks[:,...]
    slice x1, local copies, waits for them, and re-layouts: 0.01 us -> 2.39 us  [shards(): y, x, z, mass = (values[:, :, k] for k in range(4))]
    pallas_call x1, Pallas kernels: 38.2 us -> 36.9 us  [shards(): pl.pallas_call(functools.partial(density_kernel, rooms), out_shape=jax.Sh...]
    another operation x1, local copies, waits for them, and re-layouts: 0.01 us -> 0.76 us  [shards(): jnp.stack([positions[0, 0, :, 0], positions[1, 0, :, 0], positions[2, 0,...]
    iota x0 -> x10, local copies, waits for them, and re-layouts: none -> 0.75 us  [shards(): which = lax.broadcasted_iota(jnp.int32, y.shape, 0)]
    another operation x2, other arithmetic: 0.77 us -> 1.48 us  [shards(): jnp.stack([positions[0, 0, :, 0], positions[1, 0, :, 0], positions[2, 0,...]
where the time goes in v4:
time: 68.5 us; the launch traced here: 67.9 us
  Pallas kernels  49.6 us (72%)
  other arithmetic  8.71 us (13%)
  local copies, waits for them, and re-layouts  8.45 us (12%)
  between operations  0.87 us (1%)
    pallas_call x1, Pallas kernels, shards(): pl.pallas_call(functools.partial(density_kernel, rooms), out_shape=jax.Sh...  36.9 us
    pallas_call x1, Pallas kernels, halo(): pl.pallas_call(halo_kernel, out_shape=jax.ShapeDtypeStruct((3, 3) + data....  12.7 us
    select_n x1, other arithmetic, shards(): jnp.where(chosen[:, 0], ranks[:, 0] - 1, jnp.where(chosen[:, 1], ranks[:,...  3.61 us
    slice x1, local copies, waits for them, and re-layouts, shards(): y, x, z, mass = (values[:, :, k] for k in range(4))  2.39 us
    another operation x2, other arithmetic, shards(): jnp.stack([positions[0, 0, :, 0], positions[1, 0, :, 0], positions[2, 0,...  1.48 us

profile of v4, /device:TPU:0, one launch (start us, length us, event | category | flops | bytes accessed | tf_op | source)
XLA Modules:
  0.0 67.9 jit_solution(10550806807726668139)
XLA Ops:
  0.0 0.7 copy-done
  0.7 0.8 %fusion.23 = f32[16,1,256]{2,1,0:T(1,128)S(1)} fusion(f32[1,16,1,256]{3,2,1,0:T(1,128)} %param.5, s32[16]{0:T(128)S(1)} %bitcast.114), kind=kLoop, calls=%fused_computation.60 | loop fusion | flops 8192 | bytes 32832 | tf_op jit(solution)/shard_map/stack;squeeze | solution.py:226
  1.5 0.8 %slice_bitcast_fusion.4 = (f32[16,1,256]{2,1,0:T(1,128)S(1)}, f32[16,1,256]{2,1,0:T(1,128)S(1)}, f32[16,1,256]{2,1,0:T(1,128)S(1)}) fusion(f32[3,1,16,1,256]{4,3,2,1,0:T(1,128)} %param.4), kind=kLoop, calls=%fused_computation.64 | loop fusion | bytes 98304 | tf_op jit(solution)/shard_map/stack;squeeze | solution.py:226
  2.2 0.7 %pad_maximum_fusion.data_ref = f32[16,4,256]{2,1,0:T(4,128)} fusion(f32[16,1,256]{2,1,0:T(1,128)S(1)} %fusion.23, f32[16,1,256]{2,1,0:T(1,128)S(1)} %get-tuple-element.26, f32[16,1,256]{2,1,0:T(1,128)S(1)} %get-tuple-element.27, f32[16,1,256]{2,1,0:T(1,128)S(1)} %get-tuple-element.25), kind=kLoop, calls=%fused_computation.53 | loop fusion | flops 49152 | bytes 131072 | tf_op jit(solution)/shard_map/stack | solution.py:226
  2.9 12.7 %halo.1 = f32[3,3,16,4,256]{4,3,2,1,0:T(4,128)} custom-call(f32[16,4,256]{2,1,0:T(4,128)} %pad_maximum_fusion.data_ref), custom_call_target="tpu_custom_call" | custom-call | tf_op jit(solution)/shard_map/halo/pallas_call | solution.py:54
  15.6 2.4 %fusion.34 = (f32[9,16,1,256]{3,2,1,0:T(1,128)S(1)}, f32[9,16,1,256]{3,2,1,0:T(1,128)S(1)}, f32[9,16,1,256]{3,2,1,0:T(1,128)S(1)}, f32[9,16,1,256]{3,2,1,0:T(1,128)S(1)}) fusion(f32[9,16,4,256]{3,2,1,0:T(4,128)} %bitcast.99), kind=kLoop, calls=%fused_computation.103 | loop fusion | bytes 1179648 | tf_op jit(solution)/shard_map/slice | solution.py:238
  18.1 0.2 bitcast_and_fusion
  18.3 0.2 convolution_convert_fusion
  18.6 0.1 slice_add_fusion
  18.7 0.2 copy.98
  19.7 0.1 add_select_fusion
  19.8 1.1 %select_reduce_fusion.2 = (s32[16,9,3]{0,2,1:T(4,128)S(1)}, s32[16,9,3]{0,2,1:T(4,128)S(1)}) fusion(s32[9,16]{1,0:T(8,128)S(1)} %bitcast.111, s32[16,9,3]{0,2,1:T(4,128)S(1)} %add_select_fusion, s32[9,16]{1,0:T(8,128)S(1)} %bitcast.112), kind=kLoop, calls=%fused_computation.20 | loop fusion | flops 33696 | bytes 6336 | tf_op jit(solution)/shard_map/reduce_sum | solution.py:268
  21.8 0.1 iota.206
  21.9 0.2 reduce_window_sum.11
  22.3 0.3 select_reduce_fusion
  22.6 0.6 broadcast_add_fusion.list_ref
  23.2 0.2 fusion.31
  23.4 0.6 and_select_fusion.3.chunks_ref
  24.0 0.6 reshape.726.used_ref
  24.7 0.1 sub.108
  25.1 0.2 sub.110
  26.0 3.6 %and_select_fusion.1.pos_ref = s32[144,1,256]{2,1,0:T(1,128)} fusion(s32[144,1,256]{2,1,0:T(1,128)S(1)} %sub.108, pred[144,1,256]{2,0,1:T(8,128)(4,1)S(1)} %bitcast.103, pred[144,1,256]{2,0,1:T(8,128)(4,1)S(1)} %bitcast.109, pred[144,1,256]{2,0,1:T(8,128)(4,1)S(1)} %bitcast.108, pred[144,1,256]{2,0,1:T(8,128)(4,1)S(1)} %bitcast.107, ...), kind=kLoop, calls=%fused_computation.14 | loop fusion | flops 811008 | bytes 666720 | tf_op jit(solution)/shard_map/jit(_where)/select_n | solution.py:256
  29.6 36.9 %density.1 = f32[16,256]{1,0:T(8,128)} custom-call(s32[16,512]{1,0:T(8,128)} %broadcast_add_fusion.list_ref, s32[16]{0:T(128)} %and_select_fusion.3.chunks_ref, s32[16]{0:T(128)} %bitcast.113, s32[144]{0:T(256)} %reshape.726.used_ref, s32[144,1,256]{2,1,0:T(1,128)} %and_select_fusion.1.pos_ref, f32[144,4,256]{2,1,0:T(4,128)} %bitcast.100), custom_call_target="tpu_custom_call" | custom-call | tf_op jit(solution)/shard_map/density/pallas_call | solution.py:291
  66.5 1.3 %copy.88 = f32[1,16,1,256]{3,2,1,0:T(1,128)} copy(f32[1,16,1,256]{3,1,2,0:T(8,128)} %bitcast.110) | data formatting | bytes 32768 | tf_op jit(solution)/shard_map/reshape | solution.py:305
  (52 shorter events, 2.3 us)
Async XLA Ops:
  0.0 0.7 copy-start
